TPU v7x, 32 devices: a whole 2x2x4 slice. The times are simulated.
32 devices in a mesh: sp: 4 (over z), bn: 2 (over x), dp: 4 (over y, core).
Axes of the slice: x: 2, y: 2, z: 4, core: 2. Of those that a mesh axis runs over, the one named last changes fastest.
Arguments:
- images: bfloat16 [8, 4, 64, 40, 128], P(('bn', 'dp'), 'sp'), may hold values from -8 to 8, as said below
- out_grad: bfloat16 [8, 4, 256, 40, 128], P(('bn', 'dp'), 'sp'), may hold values from -8 to 8, as said below
- conv_weight: bfloat16 [3, 3, 64, 64], replicated, may hold values from -0.25 to 0.25
- proj_weight: bfloat16 [64, 256], replicated, may hold values from -0.75 to 0.75
- gain_one: float32 [64], replicated, may hold values from 0.1 to 1.9
- shift_one: float32 [64], replicated, may hold values from -3 to 3
- gain_three: float32 [256], replicated, may hold values from 0.1 to 1.9
- shift_three: float32 [256], replicated, may hold values from -3 to 3
Outputs:
- images_grad: bfloat16 [8, 4, 64, 40, 128], P(('bn', 'dp'), 'sp')
- conv_grad: float32 [3, 3, 64, 64], replicated
- proj_grad: float32 [64, 256], replicated
- gain_one_grad: float32 [64], replicated
- shift_one_grad: float32 [64], replicated
- gain_three_grad: float32 [256], replicated
- shift_three_grad: float32 [256], replicated
Inputs may be any that keep to these rules, and one draw needn't show every extreme that they name: `images`: channels of one quadrant have their own offset and spread. `out_grad`: channels of one quadrant have their own offset and spread.
All inputs are finite; a program needn't handle non-finite values.
Results may differ from a plain program's by a relative error of at most 0.029.
Values may be sent and summed in bfloat16 or wider, within the bound.
No kernel may reach another device: no remote copies, remote signals or barrier semaphores. Data moves between devices by JAX's collectives and lax.ppermute only.
A program may use at most 64 MiB of HBM per device.

v0:
```python
from functools import partial

import jax
import jax.numpy as jnp
from jax import lax
from jax.experimental import pallas as pl
from jax.experimental.pallas import tpu as pltpu
from jax.sharding import PartitionSpec as P


norm_floor = 1e-05
bf16 = jnp.bfloat16
f32 = jnp.float32
EDGE, LINES, CONV, HIDDEN, SLOPE, WIDE, GRAD, PACK, BACK = 8, 16, 14, 12, 16, 24, 20, 4, 12
group_axes = ("sp", "bn")
all_axes = ("sp", "bn", "dp")


def from_partner(value, mask):
    return lax.ppermute(value, "sp", [(i, i ^ mask) for i in range(lax.axis_size("sp"))])


def nt_dot(left, right):
    return lax.dot_general(left, right, (((1,), (1,)), ((), ())), preferred_element_type=f32)


def nn_dot(left, right):
    return lax.dot_general(left, right, (((1,), (0,)), ((), ())), preferred_element_type=f32)


def lane_pair(ref, row):
    return jnp.concatenate([ref[row], ref[row + 1]], axis=1)


def fold_pair(value):
    half = value.shape[1] // 2
    return value[:, :half] + value[:, half:]


def row_of(partials):
    depth = partials.shape[0]
    if depth < 128:
        partials = jnp.concatenate([partials, jnp.zeros((128 - depth, 128), f32)], axis=0)
    pieces = [
        jnp.sum(jnp.transpose(partials[k : k + 128]), axis=0, keepdims=True)
        for k in range(0, partials.shape[0], 128)
    ]
    return pieces[0] if len(pieces) == 1 else jnp.concatenate(pieces, axis=1)


def columns_of(rows, depth):
    width = rows[0].shape[1]
    stacked = jnp.concatenate(rows + [jnp.zeros((128 - len(rows), width), f32)], axis=0)
    pieces = [jnp.transpose(stacked[:, k : k + 128]) for k in range(0, width, 128)]
    tall = pieces[0] if len(pieces) == 1 else jnp.concatenate(pieces, axis=0)
    return [tall[:depth, k : k + 1] for k in range(len(rows))]


def pack_rows(out_ref, rows):
    devices, height, width = out_ref.shape
    lines = [row[:, k : k + width] for row in rows for k in range(0, row.shape[1], width)]
    lines += [jnp.zeros((height - len(lines), width), f32)] if len(lines) < height else []
    block = jnp.concatenate(lines, axis=0)
    for d in range(devices):
        out_ref[d] = block


def row_at(gathered_ref, device, kind, depth):
    steps = max(depth // 128, 1)
    lines = [gathered_ref[device, k : k + 1, :] for k in range(kind * steps, (kind + 1) * steps)]
    return lines[0] if steps == 1 else jnp.concatenate(lines, axis=1)


def joined_moments(gathered_ref, local_cells, depth):
    devices = gathered_ref.shape[0]
    means = [row_at(gathered_ref, d, 0, depth) for d in range(devices)]
    average = sum(means[1:], means[0]) * (1.0 / devices)
    squares = None
    for d in range(devices):
        delta = means[d] - average
        term = row_at(gathered_ref, d, 1, depth) + local_cells * (delta * delta)
        squares = term if squares is None else squares + term
    return average, squares * (1.0 / (devices * local_cells))


def summed_rows(gathered_ref, kind, depth):
    total = row_at(gathered_ref, 0, kind, depth)
    for d in range(1, gathered_ref.shape[0]):
        total = total + row_at(gathered_ref, d, kind, depth)
    return total


def logistic(value):
    return 0.5 * jnp.tanh(0.5 * value) + 0.5


def place_flags():
    position = lax.axis_index("sp")
    return position % 2, position // 2


def edge_pieces(line_of, rows, shape, row_ref, col_ref, corner_ref, at=0):
    depth, cols = shape
    column, half = place_flags()
    lane = lax.broadcasted_iota(jnp.int32, (depth, cols), 1)
    edge = jnp.where(column == 0, cols - 1, 0)

    def body(h, found):
        moved = pltpu.roll(line_of(h), lax.rem(h + 1 - edge + cols, cols), 1)
        return jnp.where(lane == h + 1, moved, found)

    kind = row_ref.dtype
    block = pl.ds(at, depth)
    found = lax.fori_loop(0, rows, body, jnp.zeros((depth, cols), f32), unroll=4)
    col_ref[block] = found.astype(kind)
    border = line_of(jnp.where(half == 0, rows - 1, 0))
    row_ref[block] = border.astype(kind)
    target = jnp.where(half == 0, 0, rows + 1)
    moved = pltpu.roll(border, lax.rem(target - edge + cols, cols), 1)
    corner_ref[block] = jnp.where(lane == target, moved, 0.0).astype(kind)


def three_shifts(line_of, border, side, out_ref):
    rows = out_ref.shape[0] - 2
    depth, cols = border.shape
    column, half = place_flags()
    lane = lax.broadcasted_iota(jnp.int32, (depth, cols), 1)
    left = jnp.where(column == 1, side, 0.0)
    right = jnp.where(column == 0, side, 0.0)

    def place(r, line):
        before = pltpu.roll(line, 1, 1)
        after = pltpu.roll(line, cols - 1, 1)
        edge_left = pltpu.roll(left, (cols - r) % cols, 1)
        edge_right = pltpu.roll(right, (2 * cols - 1 - r) % cols, 1)
        before = jnp.where(lane == 0, edge_left, before)
        after = jnp.where(lane == cols - 1, edge_right, after)
        out_ref[r] = jnp.concatenate([before, line, after], axis=0).astype(bf16)

    place(0, jnp.where(half == 1, border, 0.0))
    place(rows + 1, jnp.where(half == 0, border, 0.0))

    def body(h, carry):
        place(h + 1, line_of(h))
        return carry

    lax.fori_loop(0, rows, body, 0, unroll=4)


def conv_pair(weights, shifted_ref, row):
    depth3 = shifted_ref.shape[1]
    cols = shifted_ref.shape[2]
    first = shifted_ref[pl.ds(row, 3)].reshape(3 * depth3, cols)
    second = shifted_ref[pl.ds(row + 1, 3)].reshape(3 * depth3, cols)
    return nn_dot(weights, jnp.concatenate([first, second], axis=1))


def to_lines(planes_ref, out_ref, tall_ref):
    depth, rows, _ = planes_ref.shape
    block = tall_ref.shape[0] // rows
    for start in range(0, depth, block):

        def spill(c, carry, start=start):
            at = pl.multiple_of(c * rows, 8)
            tall_ref[pl.ds(at, rows), :] = planes_ref[start + c].astype(f32)
            return carry

        lax.fori_loop(0, block, spill, 0, unroll=8)

        def collect(h, carry, start=start):
            line = tall_ref[pl.ds(h, block, stride=rows), :]
            out_ref[h, start : start + block] = line.astype(bf16)
            return carry

        lax.fori_loop(0, rows, collect, 0, unroll=4)


def edge_kernel(planes_ref, lines_ref, row_ref, col_ref, corner_ref, tall_ref):
    rows, depth, cols = lines_ref.shape
    to_lines(planes_ref, lines_ref, tall_ref)
    edge_pieces(
        lambda h: lines_ref[h].astype(f32), rows, (depth, cols), row_ref, col_ref, corner_ref
    )


def lines_kernel(planes_ref, lines_ref, tall_ref):
    to_lines(planes_ref, lines_ref, tall_ref)


def weights_kernel(conv_ref, proj_ref, ahead_ref, behind_ref, across_ref):
    depth, wide = proj_ref.shape
    blank = jnp.zeros((depth, 128 - depth), f32)

    def turned(block):
        block = jnp.concatenate([block, blank], axis=1) if depth < 128 else block
        tall = jnp.zeros((128 - depth, 128), f32)
        block = jnp.concatenate([block, tall], axis=0) if depth < 128 else block
        return jnp.transpose(block)[:depth, :depth]

    forth, back = [], []
    for a in range(3):
        for b in range(3):
            forth.append(conv_ref[a, b])
            back.append(turned(conv_ref[2 - a, 2 - b].astype(f32)).astype(bf16))
    ahead_ref[...] = jnp.concatenate(forth, axis=1)
    behind_ref[...] = jnp.concatenate(back, axis=1)
    for k in range(0, wide, 128):
        block = proj_ref[:, k : k + 128].astype(f32)
        block = jnp.concatenate([block, jnp.zeros((128 - depth, 128), f32)], axis=0)
        across_ref[k : k + 128] = jnp.transpose(block)[:, :depth].astype(bf16)


def conv_kernel(x_ref, row_ref, col_ref, corner_ref, w_ref, a_ref, stat_ref, shifted_ref):
    rows, depth, cols = x_ref.shape
    side = col_ref[...].astype(f32) + corner_ref[...].astype(f32)
    three_shifts(lambda h: x_ref[h].astype(f32), row_ref[...].astype(f32), side, shifted_ref)
    weights = w_ref[...]

    def body(j, total):
        h = 2 * j
        both = conv_pair(weights, shifted_ref, h)
        a_ref[h] = both[:, :cols]
        a_ref[h + 1] = both[:, cols:]
        return total + fold_pair(both)

    total = lax.fori_loop(0, rows // 2, body, jnp.zeros((depth, cols), f32), unroll=4)
    mean = jnp.sum(total, axis=1, keepdims=True) * (1.0 / (rows * cols))

    def spread(h, squares):
        centred = a_ref[h] - mean
        return squares + centred * centred

    squares = lax.fori_loop(0, rows, spread, jnp.zeros((depth, cols), f32), unroll=4)
    pack_rows(stat_ref, [row_of(total) * (1.0 / (rows * cols)), row_of(squares)])


def wide_row(ref):
    row = ref[...]
    short = -row.shape[1] % 128
    return jnp.concatenate([row, jnp.zeros((1, short), f32)], axis=1) if short else row


def norm_columns(gathered_ref, gain_ref, shift_ref, local_cells):
    depth = gain_ref.shape[1]
    average, variance = joined_moments(gathered_ref, local_cells, depth)
    scale = lax.rsqrt(variance + norm_floor)
    return columns_of([average, scale, wide_row(gain_ref), wide_row(shift_ref)], depth)


def spread_column(column, cols):
    return jnp.broadcast_to(column, (column.shape[0], cols))


def hidden_kernel(a_ref, stat_ref, gain_ref, shift_ref, w_ref, y_ref, out_ref, centred_ref):
    rows, depth, cols = a_ref.shape
    cells = float(rows * cols)
    mean, scale, gain, shift = norm_columns(stat_ref, gain_ref, shift_ref, cells)
    steep = spread_column(0.5 * gain * scale, cols)
    mean = spread_column(mean, cols)
    lift = spread_column(0.5 * shift, cols)
    middle = spread_column(shift * logistic(shift), cols).astype(bf16).astype(f32)

    def activate(h, total):
        half = (a_ref[h] - mean) * steep + lift
        hidden = (half + half * jnp.tanh(half)).astype(bf16)
        y_ref[h] = hidden
        centred = hidden.astype(f32) - middle
        centred_ref[h] = centred.astype(bf16)
        return total + centred

    total = lax.fori_loop(0, rows, activate, jnp.zeros((depth, cols), f32), unroll=4)
    gram = jnp.zeros((depth, depth), f32)
    step = 8
    for h in range(0, rows, step):
        wide_lines = jnp.concatenate([centred_ref[k] for k in range(h, min(h + step, rows))], axis=1)
        gram = gram + nt_dot(wide_lines, wide_lines)
    weights = w_ref[...].astype(f32)
    mean_c = jnp.sum(total, axis=1, keepdims=True) * (1.0 / cells)
    mean_r = row_of(total)[:, :depth] * (1.0 / cells)
    spread = gram - cells * (mean_c * mean_r)
    mixed = lax.dot_general(
        spread, weights, (((1,), (0,)), ((), ())),
        precision=lax.Precision.HIGHEST, preferred_element_type=f32,
    )
    squares = jnp.maximum(jnp.sum(mixed * weights, axis=0, keepdims=True), 0.0)
    means = jnp.sum(weights * (mean_c + middle[:, 0:1]), axis=0, keepdims=True)
    pack_rows(out_ref, [means, squares])


def slope_kernel(
    y_ref, g_ref, stat_ref, gain_ref, shift_ref, w_ref, e_ref, out_ref, keep_ref
):
    rows, _, cols = y_ref.shape
    wide = w_ref.shape[0]
    mean, scale, gain, shift = norm_columns(stat_ref, gain_ref, shift_ref, float(rows * cols))
    steep = 0.5 * gain * scale
    keep_ref[0] = spread_column(mean, cols)
    keep_ref[1] = spread_column(steep, cols)
    keep_ref[2] = spread_column(0.5 * shift, cols)
    keep_ref[3] = jnp.zeros((wide, cols), f32)
    keep_ref[4] = jnp.zeros((wide, cols), f32)
    block = 128

    def body(j, carry):
        h = 2 * j
        lines = lane_pair(y_ref, h)
        for start in range(0, wide, block):
            part = slice(start, start + block)
            both = nn_dot(w_ref[part], lines)
            m, s, b = keep_ref[0, part], keep_ref[1, part], keep_ref[2, part]
            total = cross = None
            for k in range(2):
                half = (both[:, k * cols : (k + 1) * cols] - m) * s + b
                t = jnp.tanh(half)
                slope = (1.0 + t) * (1.0 + half * (1.0 - t))
                grad = g_ref[h + k, part].astype(f32) * slope
                e_ref[h + k, part] = grad.astype(bf16)
                across = grad * half
                total = grad if total is None else total + grad
                cross = across if cross is None else cross + across
            keep_ref[3, part] += total
            keep_ref[4, part] += cross
        return carry

    lax.fori_loop(0, rows // 2, body, 0, unroll=2)
    total = row_of(keep_ref[3]) * 0.5
    cross = row_of(keep_ref[4])
    pack_rows(out_ref, [total, (cross - shift_ref[...] * total) / gain_ref[...]])


def wide_kernel(
    y_ref, e_ref, a_ref, stat1_ref, gain1_ref, shift1_ref, stat3_ref, gain3_ref, shift3_ref,
    sums_ref, w_ref, wt_ref,
    e1_ref, n1_ref, out_ref, proj_ref, row_ref, col_ref, corner_ref, keep_ref, db_ref,
):
    rows, depth, cols = y_ref.shape
    wide = w_ref.shape[0]
    local_cells = float(rows * cols)
    cells = local_cells * sums_ref.shape[0]
    mean3, scale3, gain3, _ = norm_columns(stat3_ref, gain3_ref, shift3_ref, local_cells)
    mean1, scale1, gain1, shift1 = norm_columns(stat1_ref, gain1_ref, shift1_ref, local_cells)
    total3, cross3 = columns_of(
        [summed_rows(sums_ref, 0, wide), summed_rows(sums_ref, 1, wide)], wide
    )
    front = gain3 * scale3
    tilt = front * scale3 * cross3 * (1.0 / cells)
    keep_ref[0] = spread_column(0.5 * front, cols)
    keep_ref[1] = spread_column(tilt, cols)
    keep_ref[2] = spread_column(front * total3 * (1.0 / cells) - tilt * mean3, cols)
    mean1 = spread_column(mean1, cols)
    scale1 = spread_column(scale1, cols)
    gain1 = spread_column(0.5 * gain1, cols)
    shift1 = spread_column(0.5 * shift1, cols)
    weights_t = wt_ref[...]
    block = 128

    def widen(j, carry):
        h = 2 * j
        hidden = lane_pair(y_ref, h)
        for start in range(0, wide, block):
            part = slice(start, start + block)
            both = nn_dot(w_ref[part], hidden)
            p, q, r = keep_ref[0, part], keep_ref[1, part], keep_ref[2, part]
            for k in range(2):
                grad = p * e_ref[h + k, part].astype(f32) - q * both[:, k * cols : (k + 1) * cols]
                db_ref[h + k, part] = (grad - r).astype(bf16)
        return carry

    lax.fori_loop(0, rows // 2, widen, 0, unroll=2)

    def narrow(j, carry):
        total, cross = carry
        h = 2 * j
        back = nn_dot(weights_t, lane_pair(db_ref, h))
        for k in range(2):
            normed = (a_ref[h + k] - mean1) * scale1
            half = gain1 * normed + shift1
            t = jnp.tanh(half)
            slope = (0.5 + 0.5 * t) * (1.0 + half * (1.0 - t))
            grad = back[:, k * cols : (k + 1) * cols] * slope
            e1_ref[h + k] = grad.astype(bf16)
            n1_ref[h + k] = normed.astype(bf16)
            total = total + grad
            cross = cross + grad * normed
        return total, cross

    zero = jnp.zeros((depth, cols), f32)
    total, cross = lax.fori_loop(0, rows // 2, narrow, (zero, zero), unroll=4)
    pack_rows(out_ref, [row_of(total), row_of(cross)])
    for ref, at in ((e1_ref, 0), (n1_ref, depth)):
        edge_pieces(
            lambda h, ref=ref: ref[h].astype(f32), rows, (depth, cols),
            row_ref, col_ref, corner_ref, at,
        )
    proj_ref[...] = jnp.zeros(proj_ref.shape, f32)
    step = 8
    for start in range(0, rows, step):
        lines = range(start, min(start + step, rows))
        left = jnp.concatenate([y_ref[h] for h in lines], axis=1)
        right = jnp.concatenate([db_ref[h] for h in lines], axis=1)
        proj_ref[...] += nt_dot(left, right)


def corr_kernel(
    e1_ref, n1_ref, x_ref, row_ref, col_ref, corner_ref, out_ref, padded_ref, shifted_ref
):
    rows, depth, cols = e1_ref.shape
    side = col_ref[...].astype(f32) + corner_ref[...].astype(f32)
    three_shifts(lambda h: x_ref[h].astype(f32), row_ref[...].astype(f32), side, shifted_ref)
    tall = padded_ref.shape[1]
    blank = jnp.zeros((2, tall, cols), bf16)
    padded_ref[pl.ds(0, 2)] = blank
    padded_ref[pl.ds(rows + 2, 2)] = blank
    ones = jnp.ones((tall - 2 * depth, cols), bf16)

    def fill(h, carry):
        padded_ref[h + 2] = jnp.concatenate(
            [e1_ref[h], n1_ref[h], ones], axis=0
        )
        return carry

    lax.fori_loop(0, rows, fill, 0, unroll=4)
    step = 6
    total = jnp.zeros(out_ref.shape, f32)
    out_ref[...] = total
    for start in range(0, rows + 2, step):
        lines = range(start, min(start + step, rows + 2))
        left = jnp.concatenate(
            [padded_ref[pl.ds(r, 3)].reshape(3 * tall, cols) for r in lines], axis=1
        )
        right = jnp.concatenate([shifted_ref[r] for r in lines], axis=1)
        out_ref[...] += nt_dot(left, right)


def first_backward(stat1_ref, gain1_ref, sums1_ref, local_cells):
    depth = gain1_ref.shape[1]
    cells = local_cells * sums1_ref.shape[0]
    _, scale1, gain1, _ = norm_columns(stat1_ref, gain1_ref, gain1_ref, local_cells)
    sums_one = [summed_rows(sums1_ref, 0, depth), summed_rows(sums1_ref, 1, depth)]
    total1, cross1 = columns_of(sums_one, depth)
    return gain1 * scale1, total1 * (1.0 / cells), cross1 * (1.0 / cells), sums_one


def pack_kernel(
    corr_ref, stat1_ref, gain1_ref, sums1_ref, sums3_ref, proj_ref, out_ref, *, local_cells
):
    depth = proj_ref.shape[0]
    group = sums1_ref.shape[0]
    each = corr_ref.shape[0] // 3
    front, flat, tilt, sums_one = first_backward(
        stat1_ref, gain1_ref, sums1_ref, local_cells
    )
    blocks = []
    for k in range(3):
        at = k * each
        with_e = corr_ref[at : at + depth]
        with_n = corr_ref[at + depth : at + 2 * depth]
        with_one = corr_ref[at + 2 * depth : at + 2 * depth + 1]
        blocks.append(front * (with_e - flat * with_one - tilt * with_n))
    grad = jnp.concatenate(blocks, axis=0)
    tall = 3 * depth
    out_ref[0:tall] = grad[:, :128].astype(bf16)
    rest = grad[:, 128:]
    at = tall + tall // 2
    out_ref[tall:at] = jnp.concatenate([rest[: tall // 2], rest[tall // 2 :]], axis=1).astype(bf16)
    for k in range(0, proj_ref.shape[1], 128):
        out_ref[at : at + depth] = proj_ref[:, k : k + 128].astype(bf16)
        at += depth
    lines = list(sums_one)
    for kind in range(2):
        whole = summed_rows(sums3_ref, kind, proj_ref.shape[1])
        lines += [whole[:, k : k + 128] for k in range(0, whole.shape[1], 128)]
    lines.append(jnp.zeros((8 - len(lines), 128), f32))
    small = jnp.concatenate(lines, axis=0) * (1.0 / group)
    high = small.astype(bf16).astype(f32)
    out_ref[at : at + 16] = jnp.concatenate([high, small - high], axis=0).astype(bf16)
    at += 16
    out_ref[at:] = jnp.zeros((out_ref.shape[0] - at, 128), bf16)


def back_kernel(
    e1_ref, n1_ref, row_ref, col_ref, corner_ref, stat1_ref, gain1_ref, sums1_ref, w_ref,
    out_ref, shifted_ref,
):
    rows, depth, cols = e1_ref.shape
    front, flat, tilt, _ = first_backward(
        stat1_ref, gain1_ref, sums1_ref, float(rows * cols)
    )
    front = spread_column(front, cols)
    flat = spread_column(flat, cols)
    tilt = spread_column(tilt, cols)

    def line_of(e1, n1):
        return front * (e1 - flat - n1 * tilt)

    lane = lax.broadcasted_iota(jnp.int32, (depth, cols), 1)
    _, half = place_flags()
    low = jnp.where(half == 1, 0, 1)
    high = jnp.where(half == 1, rows, rows + 1)
    side = col_ref[...].astype(f32) + corner_ref[...].astype(f32)
    side = jnp.where((lane >= low) & (lane <= high), line_of(side[:depth], side[depth:]), 0.0)
    three_shifts(
        lambda h: line_of(e1_ref[h].astype(f32), n1_ref[h].astype(f32)),
        line_of(row_ref[:depth].astype(f32), row_ref[depth:].astype(f32)), side, shifted_ref,
    )
    weights = w_ref[...]

    def body(j, carry):
        h = 2 * j
        both = conv_pair(weights, shifted_ref, h).astype(bf16)
        out_ref[h] = both[:, :cols]
        out_ref[h + 1] = both[:, cols:]
        return carry

    lax.fori_loop(0, rows // 2, body, 0, unroll=4)


def sum_kernel(parts_ref, out_ref):
    total = parts_ref[0].astype(f32)
    for d in range(1, parts_ref.shape[0]):
        total = total + parts_ref[d].astype(f32)
    total = total.astype(bf16)
    for d in range(parts_ref.shape[0]):
        out_ref[d] = total


def unpack_kernel(
    in_ref, conv_ref, proj_ref, gain1_ref, shift1_ref, gain3_ref, shift3_ref, *, factor
):
    depth, wide = proj_ref.shape
    tall = 3 * depth

    def take(start, stop):
        return in_ref[start:stop].astype(f32) * factor

    main = take(0, tall)
    at = tall + tall // 2
    rest = take(tall, at)
    rest = jnp.concatenate([rest[:, :depth], rest[:, depth:]], axis=0)
    for a in range(3):
        block = main[(2 - a) * depth : (3 - a) * depth]
        conv_ref[a, 0] = block[:, :depth]
        conv_ref[a, 1] = block[:, depth:]
        conv_ref[a, 2] = rest[(2 - a) * depth : (3 - a) * depth]
    for k in range(0, wide, 128):
        proj_ref[:, k : k + 128] = take(at, at + depth)
        at += depth
    both = take(at, at + 16)
    small = both[:8] + both[8:]
    shift1_ref[...] = small[0:1, :depth]
    gain1_ref[...] = small[1:2, :depth]
    steps = wide // 128
    for ref, start in ((shift3_ref, 2), (gain3_ref, 2 + steps)):
        for k in range(steps):
            ref[:, k * 128 : (k + 1) * 128] = small[start + k : start + k + 1]


def call(kernel, mib, outs, *args, scratch=()):
    return pl.pallas_call(
        kernel,
        out_shape=[jax.ShapeDtypeStruct(s, d) for s, d in outs],
        scratch_shapes=list(scratch),
        compiler_params=pltpu.CompilerParams(vmem_limit_bytes=mib * 1024 * 1024),
    )(*args)


def exchange(row, col, corner):
    return from_partner(row, 2), from_partner(col, 1), from_partner(corner, 3)


def swap(copies, axes):
    return lax.all_to_all(copies, axes, 0, 0)


def shards(
    images, out_grad, conv_weight, proj_weight, gain_one, shift_one, gain_three, shift_three
):
    depth, rows, cols = images.shape[2:]
    wide = out_grad.shape[2]
    group = lax.axis_size(group_axes)
    devices = lax.axis_size(all_axes)
    per_image = 1.0 / float(lax.axis_size("sp") * rows * cols)
    one = gain_one.reshape(1, -1), shift_one.reshape(1, -1)
    three = gain_three.reshape(1, -1), shift_three.reshape(1, -1)
    plane = (rows, depth, cols)
    piece = ((depth, cols), bf16)
    rows_out = ((group, 8, 128), f32)

    tall = pltpu.VMEM((depth * rows, cols), f32)
    keep = [pltpu.VMEM((5, wide, cols), f32)]
    lines, *edges = call(
        edge_kernel, EDGE, [(plane, bf16)] + [piece] * 3, images[0, 0], scratch=[tall]
    )
    (cotangent,) = call(
        lines_kernel, LINES, [((rows, wide, cols), bf16)], out_grad[0, 0], scratch=[tall]
    )
    ahead, behind, proj_t = call(
        weights_kernel, 4,
        [((depth, 9 * depth), bf16)] * 2 + [((wide, depth), bf16)], conv_weight, proj_weight,
    )
    edges = exchange(*edges)
    triple = pltpu.VMEM((rows + 2, 3 * depth, cols), bf16)
    conv_out, stat = call(
        conv_kernel, CONV, [(plane, f32), rows_out], lines, *edges, ahead, scratch=[triple]
    )
    stat_one = swap(stat, group_axes)
    hidden, stat = call(
        hidden_kernel, HIDDEN, [(plane, bf16), rows_out],
        conv_out, stat_one, *one, proj_weight,
        scratch=[pltpu.VMEM(plane, bf16)],
    )
    stat_three = swap(stat, group_axes)
    grad_out, sums = call(
        slope_kernel, SLOPE, [((rows, wide, cols), bf16), rows_out],
        hidden, cotangent, stat_three, *three, proj_t, scratch=keep,
    )
    sums_three = swap(sums, group_axes)
    pieces = ((2 * depth, cols), bf16)
    grad_pre, normed, sums, proj, *last = call(
        wide_kernel, WIDE,
        [(plane, bf16), (plane, bf16), rows_out, ((depth, wide), f32)] + [pieces] * 3,
        hidden, grad_out, conv_out, stat_one, *one, stat_three, *three, sums_three,
        proj_t, proj_weight, scratch=keep + [pltpu.VMEM((rows, wide, cols), bf16)],
    )
    sums_one = swap(sums, group_axes)
    last = exchange(*last)
    each = 2 * depth + 16
    (corr,) = call(
        corr_kernel, GRAD, [((3 * each, 3 * depth), f32)],
        grad_pre, normed, lines, *edges,
        scratch=[pltpu.VMEM((rows + 4, each, cols), bf16), triple],
    )
    used = 9 * depth * depth // 128 + depth * wide // 128 + 16
    used += -used % (16 * 32)
    (part,) = call(
        partial(pack_kernel, local_cells=float(rows * cols)), PACK, [((used, 128), bf16)],
        corr, stat_one, one[0], sums_one, sums_three, proj,
    )
    (grad_field,) = call(
        back_kernel, BACK, [(plane, bf16)],
        grad_pre, normed, *last, stat_one, one[0], sums_one, behind, scratch=[triple],
    )
    part = jnp.pad(part, ((0, -used % (devices * 16)), (0, 0))).reshape(devices, -1, 128)
    parts = swap(part, all_axes)
    (mine,) = call(sum_kernel, 4, [(part.shape, bf16)], parts)
    full = swap(mine, all_axes).reshape(-1, 128)[:used]
    kernel_total, proj_total, gain1, shift1, gain3, shift3 = call(
        partial(unpack_kernel, factor=per_image), 4,
        [((3, 3, depth, depth), f32), ((depth, wide), f32)]
        + [((1, depth), f32)] * 2 + [((1, wide), f32)] * 2,
        full,
    )
    return (
        jnp.transpose(grad_field, (1, 0, 2))[None, None],
        kernel_total,
        proj_total,
        gain1[0],
        shift1[0],
        gain3[0],
        shift3[0],
    )


def solution(mesh):
    in_specs = (
        P(("bn", "dp"), "sp", None, None, None),
        P(("bn", "dp"), "sp", None, None, None),
        P(),
        P(),
        P(),
        P(),
        P(),
        P(),
    )
    out_specs = (P(("bn", "dp"), "sp", None, None, None), P(), P(), P(), P(), P(), P())
    return jax.shard_map(shards, mesh=mesh, in_specs=in_specs, out_specs=out_specs, check_vma=False)
```

profile of v0, /device:TPU:0, one launch (start us, length us, event | category | flops | bytes accessed | tf_op | source)
XLA Modules:
  0.0 105.9 jit_solution(8250202443779675102)
XLA Ops:
  0.6 0.0 copy-start.5
  0.6 1.1 %copy-done.5 = bf16[1,1,64,40,128]{4,3,2,1,0:T(8,128)(2,1)S(1)} copy-done((bf16[1,1,64,40,128]{4,3,2,1,0:T(8,128)(2,1)S(1)}, bf16[1,1,64,40,128]{4,3,2,1,0:T(8,128)(2,1)}, u32[]{:S(2)}) %copy-start.5) | copy-done | bytes 655384
  1.7 1.3 %shard_map.135 = (bf16[40,64,128]{2,1,0:T(8,128)(2,1)S(1)}, bf16[64,128]{1,0:T(8,128)(2,1)S(1)}, bf16[64,128]{1,0:T(8,128)(2,1)S(1)}, bf16[64,128]{1,0:T(8,128)(2,1)S(1)}) custom-call(bf16[64,40,128]{2,1,0:T(8,128)(2,1)S(1)} %bitcast.17), custom_call_target="tpu_custom_call" | custom-call | tf_op jit(solution)/shard_map/pallas_call | solution.py:559
  3.1 4.1 %collective-permute-start = (bf16[64,128]{1,0:T(8,128)(2,1)S(1)}, bf16[64,128]{1,0:T(8,128)(2,1)S(1)}, u32[]{:S(2)}, u32[]{:S(2)}) collective-permute-start(bf16[64,128]{1,0:T(8,128)(2,1)S(1)} %get-tuple-element.34), channel_id=1, source_target_pairs={{0,16},{8,24},{16,0},{24,8},{1,17},{9,25},{17,1},{25,9},{2,18},{10... | collective-permute-start | bytes 49160 | tf_op jit(solution)/shard_map/ppermute | solution.py:20
  7.2 1.6 %collective-permute-start.1 = (bf16[64,128]{1,0:T(8,128)(2,1)S(1)}, bf16[64,128]{1,0:T(8,128)(2,1)S(1)}, u32[]{:S(2)}, u32[]{:S(2)}) collective-permute-start(bf16[64,128]{1,0:T(8,128)(2,1)S(1)} %get-tuple-element.35), channel_id=1, source_target_pairs={{0,8},{8,0},{16,24},{24,16},{1,9},{9,1},{17,25},{25,17},{2,10},{10... | collective-permute-start | bytes 49160 | tf_op jit(solution)/shard_map/ppermute | solution.py:20
  8.7 0.0 collective-permute-start.2
  8.7 0.8 copy-done.6
  9.5 0.9 copy-done.9
  10.4 0.2 shard_map.136
  10.6 0.0 collective-permute-done.row_ref
  10.7 0.2 collective-permute-done.1.col_ref
  10.9 3.4 %collective-permute-done.2.corner_ref = bf16[64,128]{1,0:T(8,128)(2,1)S(1)} collective-permute-done((bf16[64,128]{1,0:T(8,128)(2,1)S(1)}, bf16[64,128]{1,0:T(8,128)(2,1)S(1)}, u32[]{:S(2)}, u32[]{:S(2)}) %collective-permute-start.2) | collective-permute-done | bytes 16416 | tf_op jit(solution)/shard_map/ppermute | solution.py:20
  14.3 3.6 %shard_map.137 = (f32[40,64,128]{2,1,0:T(8,128)S(1)}, f32[8,8,128]{2,1,0:T(8,128)S(1)}) custom-call(bf16[40,64,128]{2,1,0:T(8,128)(2,1)S(1)} %get-tuple-element.33.x_ref, bf16[64,128]{1,0:T(8,128)(2,1)S(1)} %collective-permute-done.row_ref, bf16[64,128]{1,0:T(8,128)(2,1)S(1)} %collective-permute-done.1.col_ref, ...), custom_call_target="tpu_custom_call" | custom-call | tf_op jit(solution)/shard_map/pallas_call | solution.py:559
  17.8 9.3 %all_to_all.30.stat_ref.stat1_ref = f32[8,8,128]{2,1,0:T(8,128)S(1)} all-to-all(f32[8,8,128]{2,1,0:T(8,128)S(1)} %get-tuple-element.39), channel_id=1, replica_groups=mesh['sp'=4,'bn'=2,'dp'=4] {'sp','bn'}, dimensions={0} | all-to-all | bytes 65536 | tf_op jit(solution)/shard_map/all_to_all | solution.py:572
  27.1 0.8 copy-done.7
  27.9 0.7 copy-done.12
  28.5 0.7 copy-done.18
  29.2 1.9 %shard_map.138 = (bf16[40,64,128]{2,1,0:T(8,128)(2,1)S(1)}, f32[8,8,128]{2,1,0:T(8,128)}) custom-call(f32[40,64,128]{2,1,0:T(8,128)S(1)} %get-tuple-element.38.a_ref, f32[8,8,128]{2,1,0:T(8,128)S(1)} %all_to_all.30.stat_ref.stat1_ref, f32[1,64]{1,0:T(1,128)S(1)} %bitcast.20, f32[1,64]{1,0:T(1,128)S(1)} %bitcast.28, bf16[64,256]{1,0:T(8,128)(2,1)S(1)} %copy-done.7), custom_call_target="tpu_custom_call" | custom-call | tf_op jit(solution)/shard_map/pallas_call | solution.py:559
  31.1 0.0 copy-done.3
  31.1 0.0 copy-done.10
  31.1 1.1 %copy-done = f32[40,64,128]{2,1,0:T(8,128)} copy-done((f32[40,64,128]{2,1,0:T(8,128)}, f32[40,64,128]{2,1,0:T(8,128)S(1)}, u32[]{:S(2)}) %copy-start) | copy-done | bytes 1310744
  32.2 3.3 %all-to-all-start.1 = ((f32[8,8,128]{2,1,0:T(8,128)}), f32[8,8,128]{2,1,0:T(8,128)S(1)}, u32[]{:S(2)}, u32[]{:S(2)}) async-start(f32[8,8,128]{2,1,0:T(8,128)} %get-tuple-element.41), calls=%async_computation.1 | async-start | bytes 65536 | tf_op jit(solution)/shard_map/all_to_all | solution.py:572
  35.6 0.0 copy-start.2
  35.6 1.7 %copy-done.2 = bf16[1,1,256,40,128]{4,3,2,1,0:T(8,128)(2,1)S(1)} copy-done((bf16[1,1,256,40,128]{4,3,2,1,0:T(8,128)(2,1)S(1)}, bf16[1,1,256,40,128]{4,3,2,1,0:T(8,128)(2,1)}, u32[]{:S(2)}) %copy-start.2) | copy-done | bytes 2621464
  37.3 1.5 %shard_map.139.g_ref = bf16[40,256,128]{2,1,0:T(8,128)(2,1)S(1)} custom-call(bf16[256,40,128]{2,1,0:T(8,128)(2,1)S(1)} %bitcast.16), custom_call_target="tpu_custom_call" | custom-call | tf_op jit(solution)/shard_map/pallas_call | solution.py:559
  38.8 0.0 copy-start.8
  38.8 3.4 %all-to-all-done.1.stat_ref.stat3_ref = f32[8,8,128]{2,1,0:T(8,128)S(1)} async-done(((f32[8,8,128]{2,1,0:T(8,128)}), f32[8,8,128]{2,1,0:T(8,128)S(1)}, u32[]{:S(2)}, u32[]{:S(2)}) %all-to-all-start.1) | async-done | bytes 32800 | tf_op jit(solution)/shard_map/all_to_all | solution.py:572
  42.2 0.8 copy-done.15
  43.0 0.7 copy-done.17
  43.7 4.4 %shard_map.140 = (bf16[40,256,128]{2,1,0:T(8,128)(2,1)S(1)}, f32[8,8,128]{2,1,0:T(8,128)S(1)}) custom-call(bf16[40,64,128]{2,1,0:T(8,128)(2,1)S(1)} %get-tuple-element.40.y_ref, bf16[40,256,128]{2,1,0:T(8,128)(2,1)S(1)} %shard_map.139.g_ref, f32[8,8,128]{2,1,0:T(8,128)S(1)} %all-to-all-done.1.stat_ref.stat3_ref, f32[1,256]{1,0:T(1,128)S(1)} %bitcast.24, ...), custom_call_target="tpu_custom_call" | custom-call | tf_op jit(solution)/shard_map/pallas_call | solution.py:559
  48.1 0.0 copy-start.4
  48.1 0.0 copy-start.11
  48.1 9.2 %all_to_all.31.sums_ref.sums3_ref = f32[8,8,128]{2,1,0:T(8,128)S(1)} all-to-all(f32[8,8,128]{2,1,0:T(8,128)S(1)} %get-tuple-element.44), channel_id=1, replica_groups=mesh['sp'=4,'bn'=2,'dp'=4] {'sp','bn'}, dimensions={0} | all-to-all | bytes 65536 | tf_op jit(solution)/shard_map/all_to_all | solution.py:572
  57.3 0.0 copy-done.8
  57.3 0.0 copy-done.1
  57.3 0.0 copy-done.13
  57.3 0.0 copy-done.16
  57.3 0.0 copy-done.19
  57.3 0.0 copy-start.14
  57.3 7.2 %shard_map.141 = (bf16[40,64,128]{2,1,0:T(8,128)(2,1)S(1)}, bf16[40,64,128]{2,1,0:T(8,128)(2,1)S(1)}, f32[8,8,128]{2,1,0:T(8,128)}, f32[64,256]{1,0:T(8,128)S(1)...) custom-call(bf16[40,64,128]{2,1,0:T(8,128)(2,1)S(1)} %get-tuple-element.40.y_ref, ...), custom_call_target="tpu_custom_call" | custom-call | tf_op jit(solution)/shard_map/pallas_call | solution.py:559
  64.5 0.6 copy-done.20
  65.1 0.6 copy-done.22
  65.8 3.5 %all-to-all-start.3 = ((f32[8,8,128]{2,1,0:T(8,128)}), f32[8,8,128]{2,1,0:T(8,128)S(1)}, u32[]{:S(2)}, u32[]{:S(2)}) async-start(f32[8,8,128]{2,1,0:T(8,128)} %get-tuple-element.50), calls=%async_computation.3 | async-start | bytes 65536 | tf_op jit(solution)/shard_map/all_to_all | solution.py:572
  69.2 0.0 copy-done.4
  69.3 0.0 copy-done.11
  69.3 3.3 %shard_map.143.corr_ref = f32[432,192]{1,0:T(8,128)S(1)} custom-call(bf16[40,64,128]{2,1,0:T(8,128)(2,1)S(1)} %get-tuple-element.45.e1_ref, bf16[40,64,128]{2,1,0:T(8,128)(2,1)S(1)} %get-tuple-element.46.n1_ref, bf16[40,64,128]{2,1,0:T(8,128)(2,1)S(1)} %copy-done.4, bf16[64,128]{1,0:T(8,128)(2,1)S(1)} %collective-permute-done.row_ref, ...), custom_call_target="tpu_custom_call" | custom-call | tf_op jit(solution)/shard_map/pallas_call | solution.py:559
  72.6 3.3 %all-to-all-done.3.sums1_ref = f32[8,8,128]{2,1,0:T(8,128)S(1)} async-done(((f32[8,8,128]{2,1,0:T(8,128)}), f32[8,8,128]{2,1,0:T(8,128)S(1)}, u32[]{:S(2)}, u32[]{:S(2)}) %all-to-all-start.3) | async-done | bytes 32800 | tf_op jit(solution)/shard_map/all_to_all | solution.py:572
  75.9 0.0 copy-done.14
  75.9 0.4 shard_map.144
  76.3 10.7 %all_to_all.32.parts_ref = bf16[32,16,128]{2,1,0:T(8,128)(2,1)S(1)} all-to-all(bf16[32,16,128]{2,1,0:T(8,128)(2,1)S(1)} %bitcast.18), channel_id=1, replica_groups=mesh['sp'=4,'bn'=2,'dp'=4] {'sp','bn','dp'}, dimensions={0} | all-to-all | bytes 262144 | tf_op jit(solution)/shard_map/all_to_all | solution.py:572
  87.0 0.7 shard_map.145
  87.7 2.6 %all-to-all-start.5 = ((bf16[32,16,128]{2,1,0:T(8,128)(2,1)}), bf16[32,16,128]{2,1,0:T(8,128)(2,1)S(1)}, u32[]{:S(2)}, u32[]{:S(2)}) async-start(bf16[32,16,128]{2,1,0:T(8,128)(2,1)} %shard_map.145), calls=%async_computation.5 | async-start | bytes 262144 | tf_op jit(solution)/shard_map/all_to_all | solution.py:572
  90.3 0.0 copy-done.23
  90.3 2.7 %collective-permute-start.3 = (bf16[128,128]{1,0:T(8,128)(2,1)S(1)}, bf16[128,128]{1,0:T(8,128)(2,1)S(1)}, u32[]{:S(2)}, u32[]{:S(2)}) collective-permute-start(bf16[128,128]{1,0:T(8,128)(2,1)S(1)} %copy-done.23), channel_id=1, source_target_pairs={{0,16},{8,24},{16,0},{24,8},{1,17},{9,25},{17,1},{25,9},{2,18},{10... | collective-permute-start | bytes 98312 | tf_op jit(solution)/shard_map/ppermute | solution.py:20
  93.0 0.0 copy-done.21
  93.0 1.5 %collective-permute-start.4 = (bf16[128,128]{1,0:T(8,128)(2,1)S(1)}, bf16[128,128]{1,0:T(8,128)(2,1)S(1)}, u32[]{:S(2)}, u32[]{:S(2)}) collective-permute-start(bf16[128,128]{1,0:T(8,128)(2,1)S(1)} %copy-done.21), channel_id=1, source_target_pairs={{0,8},{8,0},{16,24},{24,16},{1,9},{9,1},{17,25},{25,17},{2,10},{10... | collective-permute-start | bytes 98312 | tf_op jit(solution)/shard_map/ppermute | solution.py:20
  94.5 0.2 collective-permute-start.5
  94.7 4.2 %collective-permute-done.3.row_ref = bf16[128,128]{1,0:T(8,128)(2,1)S(1)} collective-permute-done((bf16[128,128]{1,0:T(8,128)(2,1)S(1)}, bf16[128,128]{1,0:T(8,128)(2,1)S(1)}, u32[]{:S(2)}, u32[]{:S(2)}) %collective-permute-start.3) | collective-permute-done | bytes 32800 | tf_op jit(solution)/shard_map/ppermute | solution.py:20
  98.9 0.0 collective-permute-done.4.col_ref
  98.9 1.3 %collective-permute-done.5.corner_ref = bf16[128,128]{1,0:T(8,128)(2,1)S(1)} collective-permute-done((bf16[128,128]{1,0:T(8,128)(2,1)S(1)}, bf16[128,128]{1,0:T(8,128)(2,1)S(1)}, u32[]{:S(2)}, u32[]{:S(2)}) %collective-permute-start.5) | collective-permute-done | bytes 32800 | tf_op jit(solution)/shard_map/ppermute | solution.py:20
  100.2 3.6 %shard_map.142 = bf16[40,64,128]{2,1,0:T(8,128)(2,1)S(1)} custom-call(bf16[40,64,128]{2,1,0:T(8,128)(2,1)S(1)} %get-tuple-element.45.e1_ref, bf16[40,64,128]{2,1,0:T(8,128)(2,1)S(1)} %get-tuple-element.46.n1_ref, bf16[128,128]{1,0:T(8,128)(2,1)S(1)} %collective-permute-done.3.row_ref, bf16[128,128]{1,0:T(8,128)(2,1)S(1)} %collective-permute-done.4.col_ref, ...), custom_call_target="tpu_custom_call" | custom-call | tf_op jit(solution)/shard_map/pallas_call | solution.py:559
  103.8 1.3 %copy.15 = bf16[1,1,64,40,128]{4,3,2,1,0:T(8,128)(2,1)} copy(bf16[1,1,64,40,128]{4,2,3,1,0:T(8,128)(2,1)S(1)} %bitcast.15) | data formatting | bytes 1310720
  105.1 0.0 all-to-all-done.5
  105.1 0.8 shard_map.146
  (18 shorter events, 0.0 us)
Async XLA Ops:
  0.6 1.1 %copy-start.5 = (bf16[1,1,64,40,128]{4,3,2,1,0:T(8,128)(2,1)S(1)}, bf16[1,1,64,40,128]{4,3,2,1,0:T(8,128)(2,1)}, u32[]{:S(2)}) copy-start(bf16[1,1,64,40,128]{4,3,2,1,0:T(8,128)(2,1)} %param.8) | copy-start | bytes 1966084
  3.1 28.1 %copy-start.3 = (bf16[40,64,128]{2,1,0:T(8,128)(2,1)}, bf16[40,64,128]{2,1,0:T(8,128)(2,1)S(1)}, u32[]{:S(2)}) copy-start(bf16[40,64,128]{2,1,0:T(8,128)(2,1)S(1)} %get-tuple-element.33.x_ref) | copy-start | bytes 1966084
  3.1 7.6 %collective-permute-start = (bf16[64,128]{1,0:T(8,128)(2,1)S(1)}, bf16[64,128]{1,0:T(8,128)(2,1)S(1)}, u32[]{:S(2)}, u32[]{:S(2)}) collective-permute-start(bf16[64,128]{1,0:T(8,128)(2,1)S(1)} %get-tuple-element.34), channel_id=1, source_target_pairs={{0,16},{8,24},{16,0},{24,8},{1,17},{9,25},{17,1},{25,9},{2,18},{10... | collective-permute-start | bytes 49160 | tf_op jit(solution)/shard_map/ppermute | solution.py:20
  7.2 3.7 %collective-permute-start.1 = (bf16[64,128]{1,0:T(8,128)(2,1)S(1)}, bf16[64,128]{1,0:T(8,128)(2,1)S(1)}, u32[]{:S(2)}, u32[]{:S(2)}) collective-permute-start(bf16[64,128]{1,0:T(8,128)(2,1)S(1)} %get-tuple-element.35), channel_id=1, source_target_pairs={{0,8},{8,0},{16,24},{24,16},{1,9},{9,1},{17,25},{25,17},{2,10},{10... | collective-permute-start | bytes 49160 | tf_op jit(solution)/shard_map/ppermute | solution.py:20
  8.7 5.5 %collective-permute-start.2 = (bf16[64,128]{1,0:T(8,128)(2,1)S(1)}, bf16[64,128]{1,0:T(8,128)(2,1)S(1)}, u32[]{:S(2)}, u32[]{:S(2)}) collective-permute-start(bf16[64,128]{1,0:T(8,128)(2,1)S(1)} %get-tuple-element.36), channel_id=1, source_target_pairs={{0,24},{8,16},{16,8},{24,0},{1,25},{9,17},{17,9},{25,1},{2,26},{10... | collective-permute-start | bytes 49160 | tf_op jit(solution)/shard_map/ppermute | solution.py:20
  8.7 0.8 copy-start.6
  9.5 0.9 copy-start.9
  14.3 16.8 %copy-start.10 = (bf16[64,128]{1,0:T(8,128)(2,1)}, bf16[64,128]{1,0:T(8,128)(2,1)S(1)}, u32[]{:S(2)}) copy-start(bf16[64,128]{1,0:T(8,128)(2,1)S(1)} %collective-permute-done.2.corner_ref) | copy-start | bytes 49156
  27.1 0.8 copy-start.7
  27.9 0.7 copy-start.12
  28.5 0.7 copy-start.18
  31.1 1.1 %copy-start = (f32[40,64,128]{2,1,0:T(8,128)}, f32[40,64,128]{2,1,0:T(8,128)S(1)}, u32[]{:S(2)}) copy-start(f32[40,64,128]{2,1,0:T(8,128)S(1)} %get-tuple-element.38.a_ref) | copy-start | bytes 3932164
  32.2 10.0 %all-to-all-start.1 = ((f32[8,8,128]{2,1,0:T(8,128)}), f32[8,8,128]{2,1,0:T(8,128)S(1)}, u32[]{:S(2)}, u32[]{:S(2)}) async-start(f32[8,8,128]{2,1,0:T(8,128)} %get-tuple-element.41), calls=%async_computation.1 | async-start | bytes 65536 | tf_op jit(solution)/shard_map/all_to_all | solution.py:572
  35.6 1.7 %copy-start.2 = (bf16[1,1,256,40,128]{4,3,2,1,0:T(8,128)(2,1)S(1)}, bf16[1,1,256,40,128]{4,3,2,1,0:T(8,128)(2,1)}, u32[]{:S(2)}) copy-start(bf16[1,1,256,40,128]{4,3,2,1,0:T(8,128)(2,1)} %param.9) | copy-start | bytes 7864324
  38.8 18.5 %copy-start.8 = (bf16[64,256]{1,0:T(8,128)(2,1)S(1)}, bf16[64,256]{1,0:T(8,128)(2,1)}, u32[]{:S(2)}) copy-start(bf16[64,256]{1,0:T(8,128)(2,1)} %wt_ref.1) | copy-start | bytes 98308
  42.2 15.1 %copy-start.1 = (f32[40,64,128]{2,1,0:T(8,128)S(1)}, f32[40,64,128]{2,1,0:T(8,128)}, u32[]{:S(2)}) copy-start(f32[40,64,128]{2,1,0:T(8,128)} %copy-done) | copy-start | bytes 3932164
  42.2 15.1 %copy-start.13 = (f32[64]{0:T(128)S(1)}, f32[64]{0:T(128)}, u32[]{:S(2)}) copy-start(f32[64]{0:T(128)} %param.12) | copy-start | bytes 772
  42.2 0.8 copy-start.15
  43.0 0.7 copy-start.17
  43.7 13.6 %copy-start.16 = (f32[256]{0:T(256)S(1)}, f32[256]{0:T(256)}, u32[]{:S(2)}) copy-start(f32[256]{0:T(256)} %param.14) | copy-start | bytes 3076
  43.7 13.7 %copy-start.19 = (f32[64]{0:T(128)S(1)}, f32[64]{0:T(128)}, u32[]{:S(2)}) copy-start(f32[64]{0:T(128)} %param.13) | copy-start | bytes 772
  48.1 21.2 %copy-start.4 = (bf16[40,64,128]{2,1,0:T(8,128)(2,1)S(1)}, bf16[40,64,128]{2,1,0:T(8,128)(2,1)}, u32[]{:S(2)}) copy-start(bf16[40,64,128]{2,1,0:T(8,128)(2,1)} %copy-done.3) | copy-start | bytes 1966084
  48.1 21.2 %copy-start.11 = (bf16[64,128]{1,0:T(8,128)(2,1)S(1)}, bf16[64,128]{1,0:T(8,128)(2,1)}, u32[]{:S(2)}) copy-start(bf16[64,128]{1,0:T(8,128)(2,1)} %copy-done.10) | copy-start | bytes 49156
  57.3 18.5 %copy-start.14 = (f32[64]{0:T(128)S(1)}, f32[64]{0:T(128)}, u32[]{:S(2)}) copy-start(f32[64]{0:T(128)} %param.12) | copy-start | bytes 772
  64.5 0.6 copy-start.20
  65.1 0.6 copy-start.22
  65.8 24.5 %copy-start.23 = (bf16[128,128]{1,0:T(8,128)(2,1)S(1)}, bf16[128,128]{1,0:T(8,128)(2,1)}, u32[]{:S(2)}) copy-start(bf16[128,128]{1,0:T(8,128)(2,1)} %copy-done.22) | copy-start | bytes 98308
  65.8 27.2 %copy-start.21 = (bf16[128,128]{1,0:T(8,128)(2,1)S(1)}, bf16[128,128]{1,0:T(8,128)(2,1)}, u32[]{:S(2)}) copy-start(bf16[128,128]{1,0:T(8,128)(2,1)} %copy-done.20) | copy-start | bytes 98308
  65.8 10.1 %all-to-all-start.3 = ((f32[8,8,128]{2,1,0:T(8,128)}), f32[8,8,128]{2,1,0:T(8,128)S(1)}, u32[]{:S(2)}, u32[]{:S(2)}) async-start(f32[8,8,128]{2,1,0:T(8,128)} %get-tuple-element.50), calls=%async_computation.3 | async-start | bytes 65536 | tf_op jit(solution)/shard_map/all_to_all | solution.py:572
  87.7 17.4 %all-to-all-start.5 = ((bf16[32,16,128]{2,1,0:T(8,128)(2,1)}), bf16[32,16,128]{2,1,0:T(8,128)(2,1)S(1)}, u32[]{:S(2)}, u32[]{:S(2)}) async-start(bf16[32,16,128]{2,1,0:T(8,128)(2,1)} %shard_map.145), calls=%async_computation.5 | async-start | bytes 262144 | tf_op jit(solution)/shard_map/all_to_all | solution.py:572
  90.3 8.6 %collective-permute-start.3 = (bf16[128,128]{1,0:T(8,128)(2,1)S(1)}, bf16[128,128]{1,0:T(8,128)(2,1)S(1)}, u32[]{:S(2)}, u32[]{:S(2)}) collective-permute-start(bf16[128,128]{1,0:T(8,128)(2,1)S(1)} %copy-done.23), channel_id=1, source_target_pairs={{0,16},{8,24},{16,0},{24,8},{1,17},{9,25},{17,1},{25,9},{2,18},{10... | collective-permute-start | bytes 98312 | tf_op jit(solution)/shard_map/ppermute | solution.py:20
  93.0 5.9 %collective-permute-start.4 = (bf16[128,128]{1,0:T(8,128)(2,1)S(1)}, bf16[128,128]{1,0:T(8,128)(2,1)S(1)}, u32[]{:S(2)}, u32[]{:S(2)}) collective-permute-start(bf16[128,128]{1,0:T(8,128)(2,1)S(1)} %copy-done.21), channel_id=1, source_target_pairs={{0,8},{8,0},{16,24},{24,16},{1,9},{9,1},{17,25},{25,17},{2,10},{10... | collective-permute-start | bytes 98312 | tf_op jit(solution)/shard_map/ppermute | solution.py:20
  94.5 5.7 %collective-permute-start.5 = (bf16[128,128]{1,0:T(8,128)(2,1)S(1)}, bf16[128,128]{1,0:T(8,128)(2,1)S(1)}, u32[]{:S(2)}, u32[]{:S(2)}) collective-permute-start(bf16[128,128]{1,0:T(8,128)(2,1)S(1)} %get-tuple-element.49), channel_id=1, source_target_pairs={{0,24},{8,16},{16,8},{24,0},{1,25},{9,17},{17,9},{25,1},{2,26},{10... | collective-permute-start | bytes 98312 | tf_op jit(solution)/shard_map/ppermute | solution.py:20
where the time goes:
time: 107 us; the launch traced here: 106 us
  blocking collectives  29.2 us (27%)
  Pallas kernels  28.9 us (27%)
  starting transfers between devices  19.5 us (18%)
  waiting for transfers between devices  15.8 us (15%)
  local copies, waits for them, and re-layouts  11.7 us (11%)
    all_to_all x3, blocking collectives, swap(): return lax.all_to_all(copies, axes, 0, 0)  29.2 us
    pallas_call x12, Pallas kernels, call(): pl.pallas_call(kernel, out_shape=[jax.ShapeDtypeStruct(s, d) for s, d in...  28.9 us
    unnamed x49, local copies, waits for them, and re-layouts  11.7 us
    ppermute x6, starting transfers between devices, from_partner(): lax.ppermute(value, 'sp', [(i, i ^ mask) for i in range(lax.axis_size('sp...  10.1 us
    all_to_all x3, starting transfers between devices, swap(): return lax.all_to_all(copies, axes, 0, 0)  9.39 us
    ppermute x6, waiting for transfers between devices, from_partner(): lax.ppermute(value, 'sp', [(i, i ^ mask) for i in range(lax.axis_size('sp...  9.13 us
    all_to_all x3, waiting for transfers between devices, swap(): return lax.all_to_all(copies, axes, 0, 0)  6.66 us
  transfers between devices with their start and end apart: 9, of which 6 were waited for; matrix products, arithmetic and copies ran while one was open for 1% of the time, Pallas kernels for 8%

commit v1 on v0

--- a/solution.py
+++ b/solution.py
@@ -11,7 +11,7 @@
 norm_floor = 1e-05
 bf16 = jnp.bfloat16
 f32 = jnp.float32
-EDGE, LINES, CONV, HIDDEN, SLOPE, WIDE, GRAD, PACK, BACK = 8, 16, 14, 12, 16, 24, 20, 4, 12
+EDGE, LINES, CONV, HIDDEN, SLOPE, WIDE, GRAD, BACK = 8, 16, 14, 12, 24, 16, 16, 12
 group_axes = ("sp", "bn")
 all_axes = ("sp", "bn", "dp")
 
@@ -65,33 +65,39 @@
         out_ref[d] = block
 
 
-def row_at(gathered_ref, device, kind, depth):
+def device_rows(gathered_ref):
+    blocks = []
+    for d in range(gathered_ref.shape[0]):
+        if gathered_ref.dtype == f32:
+            blocks.append(gathered_ref[d, 0:8])
+        else:
+            parts = gathered_ref[d, 0:32].astype(f32)
+            blocks.append(parts[0:8] + parts[8:16] + parts[16:24])
+    return blocks
+
+
+def row_at(block, kind, depth):
     steps = max(depth // 128, 1)
-    lines = [gathered_ref[device, k : k + 1, :] for k in range(kind * steps, (kind + 1) * steps)]
+    lines = [block[k : k + 1] for k in range(kind * steps, (kind + 1) * steps)]
     return lines[0] if steps == 1 else jnp.concatenate(lines, axis=1)
 
 
 def joined_moments(gathered_ref, local_cells, depth):
-    devices = gathered_ref.shape[0]
-    means = [row_at(gathered_ref, d, 0, depth) for d in range(devices)]
+    blocks = device_rows(gathered_ref)
+    devices = len(blocks)
+    means = [row_at(block, 0, depth) for block in blocks]
     average = sum(means[1:], means[0]) * (1.0 / devices)
     squares = None
-    for d in range(devices):
-        delta = means[d] - average
-        term = row_at(gathered_ref, d, 1, depth) + local_cells * (delta * delta)
+    for block, mean in zip(blocks, means):
+        delta = mean - average
+        term = row_at(block, 1, depth) + local_cells * (delta * delta)
         squares = term if squares is None else squares + term
     return average, squares * (1.0 / (devices * local_cells))
 
 
-def summed_rows(gathered_ref, kind, depth):
-    total = row_at(gathered_ref, 0, kind, depth)
-    for d in range(1, gathered_ref.shape[0]):
-        total = total + row_at(gathered_ref, d, kind, depth)
-    return total
-
-
-def logistic(value):
-    return 0.5 * jnp.tanh(0.5 * value) + 0.5
+def summed_block(gathered_ref):
+    blocks = device_rows(gathered_ref)
+    return sum(blocks[1:], blocks[0])
 
 
 def place_flags():
@@ -210,7 +216,7 @@
         across_ref[k : k + 128] = jnp.transpose(block)[:, :depth].astype(bf16)
 
 
-def conv_kernel(x_ref, row_ref, col_ref, corner_ref, w_ref, a_ref, stat_ref, shifted_ref):
+def conv_kernel(x_ref, row_ref, col_ref, corner_ref, w_ref, shifted_ref, a_ref, stat_ref):
     rows, depth, cols = x_ref.shape
     side = col_ref[...].astype(f32) + corner_ref[...].astype(f32)
     three_shifts(lambda h: x_ref[h].astype(f32), row_ref[...].astype(f32), side, shifted_ref)
@@ -251,29 +257,47 @@
     return jnp.broadcast_to(column, (column.shape[0], cols))
 
 
-def hidden_kernel(a_ref, stat_ref, gain_ref, shift_ref, w_ref, y_ref, out_ref, centred_ref):
+def hidden_kernel(
+    a_ref, stat_ref, gain_ref, shift_ref, w_ref,
+    y_ref, turn_ref, out_ref, mixed_ref, mean_ref, centred_ref,
+):
     rows, depth, cols = a_ref.shape
     cells = float(rows * cols)
     mean, scale, gain, shift = norm_columns(stat_ref, gain_ref, shift_ref, cells)
-    steep = spread_column(0.5 * gain * scale, cols)
+    gain = spread_column(0.5 * gain, cols)
+    scale = spread_column(scale, cols)
     mean = spread_column(mean, cols)
     lift = spread_column(0.5 * shift, cols)
-    middle = spread_column(shift * logistic(shift), cols).astype(bf16).astype(f32)
-
-    def activate(h, total):
-        half = (a_ref[h] - mean) * steep + lift
-        hidden = (half + half * jnp.tanh(half)).astype(bf16)
+    rest = jnp.tanh(lift)
+    middle = (lift + lift * rest).astype(bf16).astype(f32)
+    level = (0.5 + 0.5 * rest) * (1.0 + lift * (1.0 - rest))
+
+    def activate(h, carry):
+        total, turned = carry
+        normed = (a_ref[h] - mean) * scale
+        half = normed * gain + lift
+        t = jnp.tanh(half)
+        hidden = (half + half * t).astype(bf16)
+        slope = (0.5 + 0.5 * t) * (1.0 + half * (1.0 - t))
+        turn = jnp.concatenate([slope - level, slope * normed], axis=0)
+        turn_ref[h] = turn.astype(bf16)
         y_ref[h] = hidden
         centred = hidden.astype(f32) - middle
         centred_ref[h] = centred.astype(bf16)
-        return total + centred
-
-    total = lax.fori_loop(0, rows, activate, jnp.zeros((depth, cols), f32), unroll=4)
-    gram = jnp.zeros((depth, depth), f32)
+        return total + centred, turned + turn
+
+    zero = jnp.zeros((depth, cols), f32)
+    both = jnp.zeros((2 * depth, cols), f32)
+    total, turned = lax.fori_loop(0, rows, activate, (zero, both), unroll=4)
+    gram = jnp.zeros((depth, 3 * depth), f32)
     step = 8
     for h in range(0, rows, step):
-        wide_lines = jnp.concatenate([centred_ref[k] for k in range(h, min(h + step, rows))], axis=1)
-        gram = gram + nt_dot(wide_lines, wide_lines)
+        lines = range(h, min(h + step, rows))
+        left = jnp.concatenate([centred_ref[k] for k in lines], axis=1)
+        right = jnp.concatenate([turn_ref[k] for k in lines], axis=1)
+        gram = gram + nt_dot(left, jnp.concatenate([right, left], axis=0))
+    across = gram[:, : 2 * depth]
+    gram = gram[:, 2 * depth :]
     weights = w_ref[...].astype(f32)
     mean_c = jnp.sum(total, axis=1, keepdims=True) * (1.0 / cells)
     mean_r = row_of(total)[:, :depth] * (1.0 / cells)
@@ -282,15 +306,28 @@
         spread, weights, (((1,), (0,)), ((), ())),
         precision=lax.Precision.HIGHEST, preferred_element_type=f32,
     )
+    mixed_ref[...] = mixed
+    mean_ref[...] = mean_c + middle
     squares = jnp.maximum(jnp.sum(mixed * weights, axis=0, keepdims=True), 0.0)
     means = jnp.sum(weights * (mean_c + middle[:, 0:1]), axis=0, keepdims=True)
-    pack_rows(out_ref, [means, squares])
+    width = out_ref.shape[2]
+    lines = [row[:, k : k + width] for row in (means, squares) for k in range(0, row.shape[1], width)]
+    lines.append(row_of(turned))
+    block = jnp.concatenate(lines + [jnp.zeros((8 - len(lines), width), f32)], axis=0)
+    high = block.astype(bf16).astype(f32)
+    middle = (block - high).astype(bf16).astype(f32)
+    low = block - high - middle
+    block = jnp.concatenate([high, middle, low, jnp.zeros((8, width), f32), across], axis=0)
+    block = block.astype(bf16)
+    for d in range(out_ref.shape[0]):
+        out_ref[d] = block
 
 
 def slope_kernel(
-    y_ref, g_ref, stat_ref, gain_ref, shift_ref, w_ref, e_ref, out_ref, keep_ref
+    y_ref, g_ref, turn_ref, stat_ref, gain_ref, shift_ref, w_ref, wt_ref,
+    f_ref, proj_ref, out_ref, keep_ref, e_ref,
 ):
-    rows, _, cols = y_ref.shape
+    rows, depth, cols = y_ref.shape
     wide = w_ref.shape[0]
     mean, scale, gain, shift = norm_columns(stat_ref, gain_ref, shift_ref, float(rows * cols))
     steep = 0.5 * gain * scale
@@ -300,6 +337,7 @@
     keep_ref[3] = jnp.zeros((wide, cols), f32)
     keep_ref[4] = jnp.zeros((wide, cols), f32)
     block = 128
+    weights_t = wt_ref[...]
 
     def body(j, carry):
         h = 2 * j
@@ -314,7 +352,7 @@
                 t = jnp.tanh(half)
                 slope = (1.0 + t) * (1.0 + half * (1.0 - t))
                 grad = g_ref[h + k, part].astype(f32) * slope
-                e_ref[h + k, part] = grad.astype(bf16)
+                e_ref[h + k, part] = (grad * s).astype(bf16)
                 across = grad * half
                 total = grad if total is None else total + grad
                 cross = across if cross is None else cross + across
@@ -323,142 +361,127 @@
         return carry
 
     lax.fori_loop(0, rows // 2, body, 0, unroll=2)
+
+    depth2 = 2 * depth
+
+    def narrow(j, turned):
+        h = 2 * j
+        both = nn_dot(weights_t, lane_pair(e_ref, h))
+        for k in range(2):
+            line = both[:, k * cols : (k + 1) * cols]
+            f_ref[h + k] = line
+            turned = turned + jnp.concatenate([line, line], axis=0) * turn_ref[h + k].astype(f32)
+        return turned
+
+    turned = lax.fori_loop(0, rows // 2, narrow, jnp.zeros((depth2, cols), f32), unroll=4)
+    proj_ref[...] = jnp.zeros(proj_ref.shape, f32)
+    step = 8
+    for start in range(0, rows, step):
+        lines = range(start, min(start + step, rows))
+        left = jnp.concatenate([y_ref[h] for h in lines], axis=1)
+        right = jnp.concatenate([e_ref[h] for h in lines], axis=1)
+        proj_ref[...] += nt_dot(left, right)
     total = row_of(keep_ref[3]) * 0.5
     cross = row_of(keep_ref[4])
-    pack_rows(out_ref, [total, (cross - shift_ref[...] * total) / gain_ref[...]])
+    cross = (cross - shift_ref[...] * total) / gain_ref[...]
+    pack_rows(out_ref, [total, cross, row_of(turned)])
 
 
 def wide_kernel(
-    y_ref, e_ref, a_ref, stat1_ref, gain1_ref, shift1_ref, stat3_ref, gain3_ref, shift3_ref,
-    sums_ref, w_ref, wt_ref,
-    e1_ref, n1_ref, out_ref, proj_ref, row_ref, col_ref, corner_ref, keep_ref, db_ref,
+    y_ref, f_ref, a_ref, stat1_ref, gain1_ref, shift1_ref, stat3_ref, gain3_ref, sums_ref,
+    wt_ref, mixed_ref, mean_ref, part_ref,
+    da_ref, row_ref, col_ref, corner_ref, proj_ref, small_ref,
 ):
     rows, depth, cols = y_ref.shape
-    wide = w_ref.shape[0]
+    wide = wt_ref.shape[1]
     local_cells = float(rows * cols)
-    cells = local_cells * sums_ref.shape[0]
-    mean3, scale3, gain3, _ = norm_columns(stat3_ref, gain3_ref, shift3_ref, local_cells)
+    devices = sums_ref.shape[0]
+    cells = local_cells * devices
+    mean3, variance3 = joined_moments(stat3_ref, local_cells, wide)
+    scale3 = lax.rsqrt(variance3 + norm_floor)
+    front = gain3_ref[...] * scale3
+    sums = summed_block(sums_ref)
+    steps = wide // 128
+    q = front * scale3 * row_at(sums, 1, wide) * (1.0 / cells)
+    r = front * row_at(sums, 0, wide) * (1.0 / cells) - q * mean3
+    weights = wt_ref[...].astype(f32)
+    exact = lax.Precision.HIGHEST
+    mixer = lax.dot_general(
+        weights * q, weights, (((1,), (1,)), ((), ())),
+        precision=exact, preferred_element_type=f32,
+    )
+    level_row = lax.dot_general(
+        jnp.broadcast_to(r, (8, wide)), weights, (((1,), (1,)), ((), ())),
+        precision=exact, preferred_element_type=f32,
+    )[0:1]
     mean1, scale1, gain1, shift1 = norm_columns(stat1_ref, gain1_ref, shift1_ref, local_cells)
-    total3, cross3 = columns_of(
-        [summed_rows(sums_ref, 0, wide), summed_rows(sums_ref, 1, wide)], wide
-    )
-    front = gain3 * scale3
-    tilt = front * scale3 * cross3 * (1.0 / cells)
-    keep_ref[0] = spread_column(0.5 * front, cols)
-    keep_ref[1] = spread_column(tilt, cols)
-    keep_ref[2] = spread_column(front * total3 * (1.0 / cells) - tilt * mean3, cols)
+    lift = 0.5 * shift1
+    middle = (lift + lift * jnp.tanh(lift)).astype(bf16).astype(f32)
+    level_row = level_row + jnp.sum(mixer * middle, axis=0, keepdims=True)
+    across = stat3_ref[0, 32 : 32 + depth].astype(f32)
+    for d in range(1, devices):
+        across = across + stat3_ref[d, 32 : 32 + depth].astype(f32)
+    turned = summed_block(stat3_ref)[2 * steps : 2 * steps + 1]
+    double = jnp.concatenate([mixer, mixer], axis=1)
+    sums_one = sums[2 * steps : 2 * steps + 1] - jnp.sum(double * across, axis=0, keepdims=True)
+    sums_one = sums_one - jnp.concatenate([level_row, level_row], axis=1) * turned
+    blank = jnp.zeros((8 - 1 - 2 * steps, 128), f32)
+    small_ref[...] = jnp.concatenate([sums_one, sums[: 2 * steps], blank], axis=0) * (1.0 / devices)
+    (column,) = columns_of([sums_one], 2 * depth)
+    back_front = spread_column(gain1 * scale1, cols)
+    flat = spread_column(column[:depth] * (1.0 / cells), cols)
+    tilt = spread_column(column[depth:] * (1.0 / cells), cols)
+    mixer_high = mixer.astype(bf16)
+    mixer = jnp.concatenate([mixer_high, (mixer - mixer_high.astype(f32)).astype(bf16)], axis=1)
+    level = spread_column(jnp.sum(weights * r, axis=1, keepdims=True), cols)
+    mean_y = mean_ref[:, 0:1]
+    mean_b = jnp.sum(weights * mean_y, axis=0, keepdims=True)
+    proj_ref[...] = part_ref[...] - q * mixed_ref[...] - (local_cells * mean_y) * (q * mean_b + r)
     mean1 = spread_column(mean1, cols)
     scale1 = spread_column(scale1, cols)
     gain1 = spread_column(0.5 * gain1, cols)
-    shift1 = spread_column(0.5 * shift1, cols)
-    weights_t = wt_ref[...]
-    block = 128
-
-    def widen(j, carry):
+    shift1 = spread_column(lift, cols)
+
+    def narrow(j, carry):
         h = 2 * j
-        hidden = lane_pair(y_ref, h)
-        for start in range(0, wide, block):
-            part = slice(start, start + block)
-            both = nn_dot(w_ref[part], hidden)
-            p, q, r = keep_ref[0, part], keep_ref[1, part], keep_ref[2, part]
-            for k in range(2):
-                grad = p * e_ref[h + k, part].astype(f32) - q * both[:, k * cols : (k + 1) * cols]
-                db_ref[h + k, part] = (grad - r).astype(bf16)
-        return carry
-
-    lax.fori_loop(0, rows // 2, widen, 0, unroll=2)
-
-    def narrow(j, carry):
-        total, cross = carry
-        h = 2 * j
-        back = nn_dot(weights_t, lane_pair(db_ref, h))
+        lines = lane_pair(y_ref, h)
+        back = nn_dot(mixer, jnp.concatenate([lines, lines], axis=0))
         for k in range(2):
             normed = (a_ref[h + k] - mean1) * scale1
             half = gain1 * normed + shift1
             t = jnp.tanh(half)
             slope = (0.5 + 0.5 * t) * (1.0 + half * (1.0 - t))
-            grad = back[:, k * cols : (k + 1) * cols] * slope
-            e1_ref[h + k] = grad.astype(bf16)
-            n1_ref[h + k] = normed.astype(bf16)
-            total = total + grad
-            cross = cross + grad * normed
-        return total, cross
-
-    zero = jnp.zeros((depth, cols), f32)
-    total, cross = lax.fori_loop(0, rows // 2, narrow, (zero, zero), unroll=4)
-    pack_rows(out_ref, [row_of(total), row_of(cross)])
-    for ref, at in ((e1_ref, 0), (n1_ref, depth)):
-        edge_pieces(
-            lambda h, ref=ref: ref[h].astype(f32), rows, (depth, cols),
-            row_ref, col_ref, corner_ref, at,
-        )
-    proj_ref[...] = jnp.zeros(proj_ref.shape, f32)
-    step = 8
-    for start in range(0, rows, step):
-        lines = range(start, min(start + step, rows))
-        left = jnp.concatenate([y_ref[h] for h in lines], axis=1)
-        right = jnp.concatenate([db_ref[h] for h in lines], axis=1)
-        proj_ref[...] += nt_dot(left, right)
-
-
-def corr_kernel(
-    e1_ref, n1_ref, x_ref, row_ref, col_ref, corner_ref, out_ref, padded_ref, shifted_ref
-):
-    rows, depth, cols = e1_ref.shape
-    side = col_ref[...].astype(f32) + corner_ref[...].astype(f32)
-    three_shifts(lambda h: x_ref[h].astype(f32), row_ref[...].astype(f32), side, shifted_ref)
-    tall = padded_ref.shape[1]
-    blank = jnp.zeros((2, tall, cols), bf16)
+            grad = (f_ref[h + k] - back[:, k * cols : (k + 1) * cols] - level) * slope
+            da_ref[h + k] = (back_front * (grad - flat - normed * tilt)).astype(bf16)
+        return carry
+
+    lax.fori_loop(0, rows // 2, narrow, 0, unroll=4)
+    edge_pieces(
+        lambda h: da_ref[h].astype(f32), rows, (depth, cols), row_ref, col_ref, corner_ref
+    )
+
+
+def corr_kernel(da_ref, shifted_ref, proj_ref, small_ref, out_ref, padded_ref):
+    rows, depth, cols = da_ref.shape
+    blank = jnp.zeros((2, depth, cols), bf16)
     padded_ref[pl.ds(0, 2)] = blank
     padded_ref[pl.ds(rows + 2, 2)] = blank
-    ones = jnp.ones((tall - 2 * depth, cols), bf16)
 
     def fill(h, carry):
-        padded_ref[h + 2] = jnp.concatenate(
-            [e1_ref[h], n1_ref[h], ones], axis=0
-        )
+        padded_ref[h + 2] = da_ref[h]
         return carry
 
-    lax.fori_loop(0, rows, fill, 0, unroll=4)
+    lax.fori_loop(0, rows, fill, 0, unroll=8)
+    tall = 3 * depth
     step = 6
-    total = jnp.zeros(out_ref.shape, f32)
-    out_ref[...] = total
+    grad = jnp.zeros((tall, tall), f32)
     for start in range(0, rows + 2, step):
         lines = range(start, min(start + step, rows + 2))
         left = jnp.concatenate(
-            [padded_ref[pl.ds(r, 3)].reshape(3 * tall, cols) for r in lines], axis=1
+            [padded_ref[pl.ds(r, 3)].reshape(tall, cols) for r in lines], axis=1
         )
         right = jnp.concatenate([shifted_ref[r] for r in lines], axis=1)
-        out_ref[...] += nt_dot(left, right)
-
-
-def first_backward(stat1_ref, gain1_ref, sums1_ref, local_cells):
-    depth = gain1_ref.shape[1]
-    cells = local_cells * sums1_ref.shape[0]
-    _, scale1, gain1, _ = norm_columns(stat1_ref, gain1_ref, gain1_ref, local_cells)
-    sums_one = [summed_rows(sums1_ref, 0, depth), summed_rows(sums1_ref, 1, depth)]
-    total1, cross1 = columns_of(sums_one, depth)
-    return gain1 * scale1, total1 * (1.0 / cells), cross1 * (1.0 / cells), sums_one
-
-
-def pack_kernel(
-    corr_ref, stat1_ref, gain1_ref, sums1_ref, sums3_ref, proj_ref, out_ref, *, local_cells
-):
-    depth = proj_ref.shape[0]
-    group = sums1_ref.shape[0]
-    each = corr_ref.shape[0] // 3
-    front, flat, tilt, sums_one = first_backward(
-        stat1_ref, gain1_ref, sums1_ref, local_cells
-    )
-    blocks = []
-    for k in range(3):
-        at = k * each
-        with_e = corr_ref[at : at + depth]
-        with_n = corr_ref[at + depth : at + 2 * depth]
-        with_one = corr_ref[at + 2 * depth : at + 2 * depth + 1]
-        blocks.append(front * (with_e - flat * with_one - tilt * with_n))
-    grad = jnp.concatenate(blocks, axis=0)
-    tall = 3 * depth
+        grad = grad + nt_dot(left, right)
     out_ref[0:tall] = grad[:, :128].astype(bf16)
     rest = grad[:, 128:]
     at = tall + tall // 2
@@ -466,43 +489,17 @@
     for k in range(0, proj_ref.shape[1], 128):
         out_ref[at : at + depth] = proj_ref[:, k : k + 128].astype(bf16)
         at += depth
-    lines = list(sums_one)
-    for kind in range(2):
-        whole = summed_rows(sums3_ref, kind, proj_ref.shape[1])
-        lines += [whole[:, k : k + 128] for k in range(0, whole.shape[1], 128)]
-    lines.append(jnp.zeros((8 - len(lines), 128), f32))
-    small = jnp.concatenate(lines, axis=0) * (1.0 / group)
+    small = small_ref[...]
     high = small.astype(bf16).astype(f32)
     out_ref[at : at + 16] = jnp.concatenate([high, small - high], axis=0).astype(bf16)
     at += 16
     out_ref[at:] = jnp.zeros((out_ref.shape[0] - at, 128), bf16)
 
 
-def back_kernel(
-    e1_ref, n1_ref, row_ref, col_ref, corner_ref, stat1_ref, gain1_ref, sums1_ref, w_ref,
-    out_ref, shifted_ref,
-):
-    rows, depth, cols = e1_ref.shape
-    front, flat, tilt, _ = first_backward(
-        stat1_ref, gain1_ref, sums1_ref, float(rows * cols)
-    )
-    front = spread_column(front, cols)
-    flat = spread_column(flat, cols)
-    tilt = spread_column(tilt, cols)
-
-    def line_of(e1, n1):
-        return front * (e1 - flat - n1 * tilt)
-
-    lane = lax.broadcasted_iota(jnp.int32, (depth, cols), 1)
-    _, half = place_flags()
-    low = jnp.where(half == 1, 0, 1)
-    high = jnp.where(half == 1, rows, rows + 1)
+def back_kernel(d_ref, row_ref, col_ref, corner_ref, w_ref, out_ref, shifted_ref):
+    rows, _, cols = d_ref.shape
     side = col_ref[...].astype(f32) + corner_ref[...].astype(f32)
-    side = jnp.where((lane >= low) & (lane <= high), line_of(side[:depth], side[depth:]), 0.0)
-    three_shifts(
-        lambda h: line_of(e1_ref[h].astype(f32), n1_ref[h].astype(f32)),
-        line_of(row_ref[:depth].astype(f32), row_ref[depth:].astype(f32)), side, shifted_ref,
-    )
+    three_shifts(lambda h: d_ref[h].astype(f32), row_ref[...].astype(f32), side, shifted_ref)
     weights = w_ref[...]
 
     def body(j, carry):
@@ -548,9 +545,9 @@
     both = take(at, at + 16)
     small = both[:8] + both[8:]
     shift1_ref[...] = small[0:1, :depth]
-    gain1_ref[...] = small[1:2, :depth]
+    gain1_ref[...] = small[0:1, depth : 2 * depth]
     steps = wide // 128
-    for ref, start in ((shift3_ref, 2), (gain3_ref, 2 + steps)):
+    for ref, start in ((shift3_ref, 1), (gain3_ref, 1 + steps)):
         for k in range(steps):
             ref[:, k * 128 : (k + 1) * 128] = small[start + k : start + k + 1]
 
@@ -600,45 +597,40 @@
     )
     edges = exchange(*edges)
     triple = pltpu.VMEM((rows + 2, 3 * depth, cols), bf16)
-    conv_out, stat = call(
-        conv_kernel, CONV, [(plane, f32), rows_out], lines, *edges, ahead, scratch=[triple]
+    shifted, conv_out, stat = call(
+        conv_kernel, CONV,
+        [((rows + 2, 3 * depth, cols), bf16), (plane, f32), rows_out], lines, *edges, ahead,
     )
     stat_one = swap(stat, group_axes)
-    hidden, stat = call(
-        hidden_kernel, HIDDEN, [(plane, bf16), rows_out],
+    hidden, turn, stat, mixed, mean_y = call(
+        hidden_kernel, HIDDEN,
+        [(plane, bf16), ((rows, 2 * depth, cols), bf16), ((group, 32 + depth, 128), bf16)]
+        + [((depth, wide), f32), ((depth, cols), f32)],
         conv_out, stat_one, *one, proj_weight,
         scratch=[pltpu.VMEM(plane, bf16)],
     )
     stat_three = swap(stat, group_axes)
-    grad_out, sums = call(
-        slope_kernel, SLOPE, [((rows, wide, cols), bf16), rows_out],
-        hidden, cotangent, stat_three, *three, proj_t, scratch=keep,
+    narrowed, part, sums = call(
+        slope_kernel, SLOPE, [(plane, f32), ((depth, wide), f32), rows_out],
+        hidden, cotangent, turn, stat_three, *three, proj_t, proj_weight,
+        scratch=keep + [pltpu.VMEM((rows, wide, cols), bf16)],
     )
     sums_three = swap(sums, group_axes)
-    pieces = ((2 * depth, cols), bf16)
-    grad_pre, normed, sums, proj, *last = call(
+    grad_conv, *last, proj, small = call(
         wide_kernel, WIDE,
-        [(plane, bf16), (plane, bf16), rows_out, ((depth, wide), f32)] + [pieces] * 3,
-        hidden, grad_out, conv_out, stat_one, *one, stat_three, *three, sums_three,
-        proj_t, proj_weight, scratch=keep + [pltpu.VMEM((rows, wide, cols), bf16)],
-    )
-    sums_one = swap(sums, group_axes)
+        [(plane, bf16)] + [piece] * 3 + [((depth, wide), f32), ((8, 128), f32)],
+        hidden, narrowed, conv_out, stat_one, *one, stat_three, three[0], sums_three,
+        proj_weight, mixed, mean_y, part,
+    )
     last = exchange(*last)
-    each = 2 * depth + 16
-    (corr,) = call(
-        corr_kernel, GRAD, [((3 * each, 3 * depth), f32)],
-        grad_pre, normed, lines, *edges,
-        scratch=[pltpu.VMEM((rows + 4, each, cols), bf16), triple],
-    )
     used = 9 * depth * depth // 128 + depth * wide // 128 + 16
     used += -used % (16 * 32)
     (part,) = call(
-        partial(pack_kernel, local_cells=float(rows * cols)), PACK, [((used, 128), bf16)],
-        corr, stat_one, one[0], sums_one, sums_three, proj,
+        corr_kernel, GRAD, [((used, 128), bf16)], grad_conv, shifted, proj, small,
+        scratch=[pltpu.VMEM((rows + 4, depth, cols), bf16)],
     )
     (grad_field,) = call(
-        back_kernel, BACK, [(plane, bf16)],
-        grad_pre, normed, *last, stat_one, one[0], sums_one, behind, scratch=[triple],
+        back_kernel, BACK, [(plane, bf16)], grad_conv, *last, behind, scratch=[triple]
     )
     part = jnp.pad(part, ((0, -used % (devices * 16)), (0, 0))).reshape(devices, -1, 128)
     parts = swap(part, all_axes)

time: 107 us -> 99.6 us (0.931)
  Pallas kernels: 28.9 us -> 24.5 us
  local copies, waits for them, and re-layouts: 11.7 us -> 15.9 us
  waiting for transfers between devices: 15.8 us -> 12.2 us
  starting transfers between devices: 19.5 us -> 16.1 us
    pallas_call x12 -> x11, Pallas kernels: 28.9 us -> 24.5 us  [call(): pl.pallas_call(kernel, out_shape=[jax.ShapeDtypeStruct(s, d) for s, d in...]
    unnamed x49 -> x53, local copies, waits for them, and re-layouts: 11.7 us -> 15.9 us
    all_to_all x3 -> x2, starting transfers between devices: 9.39 us -> 5.97 us  [swap(): return lax.all_to_all(copies, axes, 0, 0)]
    all_to_all x3 -> x2, waiting for transfers between devices: 6.66 us -> 4.48 us  [swap(): return lax.all_to_all(copies, axes, 0, 0)]
    ppermute x6, waiting for transfers between devices: 9.13 us -> 7.7 us  [from_partner(): lax.ppermute(value, 'sp', [(i, i ^ mask) for i in range(lax.axis_size('sp...]
  transfers between devices with their start and end apart: 9 -> 8, of which waited for: 6 -> 4; matrix products, arithmetic and copies ran while one was open for 1% -> 1% of each run, Pallas kernels for 8% -> 5%
where the time goes in v1:
time: 99.6 us; the launch traced here: 98.9 us
  blocking collectives  29.4 us (30%)
  Pallas kernels  24.5 us (25%)
  starting transfers between devices  16.1 us (16%)
  local copies, waits for them, and re-layouts  15.9 us (16%)
  waiting for transfers between devices  12.2 us (12%)
    all_to_all x3, blocking collectives, swap(): return lax.all_to_all(copies, axes, 0, 0)  29.4 us
    pallas_call x11, Pallas kernels, call(): pl.pallas_call(kernel, out_shape=[jax.ShapeDtypeStruct(s, d) for s, d in...  24.5 us
    unnamed x53, local copies, waits for them, and re-layouts  15.9 us
    ppermute x6, starting transfers between devices, from_partner(): lax.ppermute(value, 'sp', [(i, i ^ mask) for i in range(lax.axis_size('sp...  10.1 us
    ppermute x6, waiting for transfers between devices, from_partner(): lax.ppermute(value, 'sp', [(i, i ^ mask) for i in range(lax.axis_size('sp...  7.7 us
    all_to_all x2, starting transfers between devices, swap(): return lax.all_to_all(copies, axes, 0, 0)  5.97 us
    all_to_all x2, waiting for transfers between devices, swap(): return lax.all_to_all(copies, axes, 0, 0)  4.48 us
  transfers between devices with their start and end apart: 8, of which 4 were waited for; matrix products, arithmetic and copies ran while one was open for 1% of the time, Pallas kernels for 5%

profile of v1, /device:TPU:0, one launch (start us, length us, event | category | flops | bytes accessed | tf_op | source)
XLA Modules:
  0.0 98.9 jit_solution(5722732679144544122)
XLA Ops:
  0.6 0.0 copy-start.7
  0.6 1.1 %copy-done.7 = bf16[1,1,64,40,128]{4,3,2,1,0:T(8,128)(2,1)S(1)} copy-done((bf16[1,1,64,40,128]{4,3,2,1,0:T(8,128)(2,1)S(1)}, bf16[1,1,64,40,128]{4,3,2,1,0:T(8,128)(2,1)}, u32[]{:S(2)}) %copy-start.7) | copy-done | bytes 655384
  1.7 1.3 %shard_map.135 = (bf16[40,64,128]{2,1,0:T(8,128)(2,1)S(1)}, bf16[64,128]{1,0:T(8,128)(2,1)S(1)}, bf16[64,128]{1,0:T(8,128)(2,1)S(1)}, bf16[64,128]{1,0:T(8,128)(2,1)S(1)}) custom-call(bf16[64,40,128]{2,1,0:T(8,128)(2,1)S(1)} %bitcast.17), custom_call_target="tpu_custom_call" | custom-call | tf_op jit(solution)/shard_map/pallas_call | solution.py:556
  3.1 4.1 %collective-permute-start = (bf16[64,128]{1,0:T(8,128)(2,1)S(1)}, bf16[64,128]{1,0:T(8,128)(2,1)S(1)}, u32[]{:S(2)}, u32[]{:S(2)}) collective-permute-start(bf16[64,128]{1,0:T(8,128)(2,1)S(1)} %get-tuple-element.38), channel_id=1, source_target_pairs={{0,16},{8,24},{16,0},{24,8},{1,17},{9,25},{17,1},{25,9},{2,18},{10... | collective-permute-start | bytes 49160 | tf_op jit(solution)/shard_map/ppermute | solution.py:20
  7.1 1.6 %collective-permute-start.1 = (bf16[64,128]{1,0:T(8,128)(2,1)S(1)}, bf16[64,128]{1,0:T(8,128)(2,1)S(1)}, u32[]{:S(2)}, u32[]{:S(2)}) collective-permute-start(bf16[64,128]{1,0:T(8,128)(2,1)S(1)} %get-tuple-element.39), channel_id=1, source_target_pairs={{0,8},{8,0},{16,24},{24,16},{1,9},{9,1},{17,25},{25,17},{2,10},{10... | collective-permute-start | bytes 49160 | tf_op jit(solution)/shard_map/ppermute | solution.py:20
  8.7 0.0 collective-permute-start.2
  8.7 0.8 copy-done.8
  9.5 0.9 copy-done.11
  10.4 0.2 shard_map.136
  10.6 0.0 copy-start.12
  10.6 0.6 copy-done.12
  11.3 0.6 copy-done.14
  11.9 0.0 collective-permute-done.row_ref
  11.9 0.0 collective-permute-done.1.col_ref
  11.9 2.4 %collective-permute-done.2.corner_ref = bf16[64,128]{1,0:T(8,128)(2,1)S(1)} collective-permute-done((bf16[64,128]{1,0:T(8,128)(2,1)S(1)}, bf16[64,128]{1,0:T(8,128)(2,1)S(1)}, u32[]{:S(2)}, u32[]{:S(2)}) %collective-permute-start.2) | collective-permute-done | bytes 16416 | tf_op jit(solution)/shard_map/ppermute | solution.py:20
  14.2 3.6 %shard_map.137 = (bf16[42,192,128]{2,1,0:T(8,128)(2,1)S(1)}, f32[40,64,128]{2,1,0:T(8,128)S(1)}, f32[8,8,128]{2,1,0:T(8,128)S(1)}) custom-call(bf16[40,64,128]{2,1,0:T(8,128)(2,1)S(1)} %get-tuple-element.37.x_ref, bf16[64,128]{1,0:T(8,128)(2,1)S(1)} %collective-permute-done.row_ref, bf16[64,128]{1,0:T(8,128)(2,1)S(1)} %collective-permute-done.1.col_ref, ...), custom_call_target="tpu_custom_call" | custom-call | tf_op jit(solution)/shard_map/pallas_call | solution.py:556
  17.8 0.0 copy-start.3
  17.8 1.3 %copy-done.3 = bf16[42,192,128]{2,1,0:T(8,128)(2,1)} copy-done((bf16[42,192,128]{2,1,0:T(8,128)(2,1)}, bf16[42,192,128]{2,1,0:T(8,128)(2,1)S(1)}, u32[]{:S(2)}) %copy-start.3) | copy-done | bytes 2064408
  19.2 10.2 %all_to_all.25.stat_ref.stat1_ref = f32[8,8,128]{2,1,0:T(8,128)S(1)} all-to-all(f32[8,8,128]{2,1,0:T(8,128)S(1)} %get-tuple-element.43), channel_id=1, replica_groups=mesh['sp'=4,'bn'=2,'dp'=4] {'sp','bn'}, dimensions={0} | all-to-all | bytes 65536 | tf_op jit(solution)/shard_map/all_to_all | solution.py:569
  29.3 0.8 copy-done.9
  30.1 0.7 copy-done.21
  30.7 0.7 copy-done.23
  31.4 3.0 %shard_map.138 = (bf16[40,64,128]{2,1,0:T(8,128)(2,1)S(1)}, bf16[40,128,128]{2,1,0:T(8,128)(2,1)S(1)}, bf16[8,96,128]{2,1,0:T(8,128)(2,1)}, f32[64,256]{1,0:T(8,128)S(1)}, f32[64,128]{1,0:T(8,128)S(1)}) custom-call(f32[40,64,128]{2,1,0:T(8,128)S(1)} %get-tuple-element.42.a_ref, f32[8,8,128]{2,1,0:T(8,128)S(1)} %all_to_all.25.stat_ref.stat1_ref, ...), custom_call_target="tpu_custom_call" | custom-call | tf_op jit(solution)/shard_map/pallas_call | solution.py:556
  34.4 1.1 %copy-done = f32[40,64,128]{2,1,0:T(8,128)} copy-done((f32[40,64,128]{2,1,0:T(8,128)}, f32[40,64,128]{2,1,0:T(8,128)S(1)}, u32[]{:S(2)}) %copy-start) | copy-done | bytes 1310744
  35.5 1.0 %copy-done.5 = bf16[40,128,128]{2,1,0:T(8,128)(2,1)} copy-done((bf16[40,128,128]{2,1,0:T(8,128)(2,1)}, bf16[40,128,128]{2,1,0:T(8,128)(2,1)S(1)}, u32[]{:S(2)}) %copy-start.5) | copy-done | bytes 1310744
  36.5 0.6 copy-done.16
  37.2 0.6 copy-done.18
  37.8 3.4 %all-to-all-start.1 = ((bf16[8,96,128]{2,1,0:T(8,128)(2,1)}), bf16[8,96,128]{2,1,0:T(8,128)(2,1)S(1)}, u32[]{:S(2)}, u32[]{:S(2)}) async-start(bf16[8,96,128]{2,1,0:T(8,128)(2,1)} %get-tuple-element.46), calls=%async_computation.1 | async-start | bytes 393216 | tf_op jit(solution)/shard_map/all_to_all | solution.py:569
  41.2 0.0 copy-start.2
  41.2 1.7 %copy-done.2 = bf16[1,1,256,40,128]{4,3,2,1,0:T(8,128)(2,1)S(1)} copy-done((bf16[1,1,256,40,128]{4,3,2,1,0:T(8,128)(2,1)S(1)}, bf16[1,1,256,40,128]{4,3,2,1,0:T(8,128)(2,1)}, u32[]{:S(2)}) %copy-start.2) | copy-done | bytes 2621464
  42.9 1.5 %shard_map.139.g_ref = bf16[40,256,128]{2,1,0:T(8,128)(2,1)S(1)} custom-call(bf16[256,40,128]{2,1,0:T(8,128)(2,1)S(1)} %bitcast.15), custom_call_target="tpu_custom_call" | custom-call | tf_op jit(solution)/shard_map/pallas_call | solution.py:556
  44.4 4.5 %all-to-all-done.1.stat_ref.stat3_ref = bf16[8,96,128]{2,1,0:T(8,128)(2,1)S(1)} async-done(((bf16[8,96,128]{2,1,0:T(8,128)(2,1)}), bf16[8,96,128]{2,1,0:T(8,128)(2,1)S(1)}, u32[]{:S(2)}, u32[]{:S(2)}) %all-to-all-start.1) | async-done | bytes 196640 | tf_op jit(solution)/shard_map/all_to_all | solution.py:569
  48.9 0.0 copy-done.10
  48.9 0.0 copy-done.20
  48.9 0.0 copy-done.25
  48.9 0.0 copy-start.6
  48.9 1.3 %copy-done.6 = bf16[40,128,128]{2,1,0:T(8,128)(2,1)S(1)} copy-done((bf16[40,128,128]{2,1,0:T(8,128)(2,1)S(1)}, bf16[40,128,128]{2,1,0:T(8,128)(2,1)}, u32[]{:S(2)}) %copy-start.6) | copy-done | bytes 1310744
  50.2 0.8 copy-done.15
  51.1 0.0 copy-start.24
  51.1 6.5 %shard_map.140 = (f32[40,64,128]{2,1,0:T(8,128)S(1)}, f32[64,256]{1,0:T(8,128)S(1)}, f32[8,8,128]{2,1,0:T(8,128)S(1)}) custom-call(bf16[40,64,128]{2,1,0:T(8,128)(2,1)S(1)} %get-tuple-element.44.y_ref, bf16[40,256,128]{2,1,0:T(8,128)(2,1)S(1)} %shard_map.139.g_ref, bf16[40,128,128]{2,1,0:T(8,128)(2,1)S(1)} %copy-done.6, ...), custom_call_target="tpu_custom_call" | custom-call | tf_op jit(solution)/shard_map/pallas_call | solution.py:556
  57.6 0.0 copy-start.4
  57.6 9.2 %all_to_all.26.sums_ref = f32[8,8,128]{2,1,0:T(8,128)S(1)} all-to-all(f32[8,8,128]{2,1,0:T(8,128)S(1)} %get-tuple-element.49), channel_id=1, replica_groups=mesh['sp'=4,'bn'=2,'dp'=4] {'sp','bn'}, dimensions={0} | all-to-all | bytes 65536 | tf_op jit(solution)/shard_map/all_to_all | solution.py:569
  66.8 0.0 copy-done.1
  66.8 0.0 copy-done.17
  66.8 0.0 copy-done.19
  66.8 0.0 copy-done.22
  66.8 0.0 copy-done.24
  66.8 2.7 %shard_map.141 = (bf16[40,64,128]{2,1,0:T(8,128)(2,1)S(1)}, bf16[64,128]{1,0:T(8,128)(2,1)S(1)}, bf16[64,128]{1,0:T(8,128)(2,1)S(1)}, bf16[64,128]{1,0:T(8,128)(...) custom-call(bf16[40,64,128]{2,1,0:T(8,128)(2,1)S(1)} %get-tuple-element.44.y_ref, ...), custom_call_target="tpu_custom_call" | custom-call | tf_op jit(solution)/shard_map/pallas_call | solution.py:556
  69.6 0.0 copy-done.4
  69.6 0.8 shard_map.143
  70.4 10.0 %all_to_all.27.parts_ref = bf16[32,16,128]{2,1,0:T(8,128)(2,1)S(1)} all-to-all(bf16[32,16,128]{2,1,0:T(8,128)(2,1)S(1)} %bitcast.18), channel_id=1, replica_groups=mesh['sp'=4,'bn'=2,'dp'=4] {'sp','bn','dp'}, dimensions={0} | all-to-all | bytes 262144 | tf_op jit(solution)/shard_map/all_to_all | solution.py:569
  80.4 0.7 shard_map.144
  81.1 2.6 %all-to-all-start.4 = ((bf16[32,16,128]{2,1,0:T(8,128)(2,1)}), bf16[32,16,128]{2,1,0:T(8,128)(2,1)S(1)}, u32[]{:S(2)}, u32[]{:S(2)}) async-start(bf16[32,16,128]{2,1,0:T(8,128)(2,1)} %shard_map.144), calls=%async_computation.4 | async-start | bytes 262144 | tf_op jit(solution)/shard_map/all_to_all | solution.py:569
  83.7 2.7 %collective-permute-start.3 = (bf16[64,128]{1,0:T(8,128)(2,1)S(1)}, bf16[64,128]{1,0:T(8,128)(2,1)S(1)}, u32[]{:S(2)}, u32[]{:S(2)}) collective-permute-start(bf16[64,128]{1,0:T(8,128)(2,1)S(1)} %get-tuple-element.54), channel_id=1, source_target_pairs={{0,16},{8,24},{16,0},{24,8},{1,17},{9,25},{17,1},{25,9},{2,18},{10... | collective-permute-start | bytes 49160 | tf_op jit(solution)/shard_map/ppermute | solution.py:20
  86.4 1.5 %collective-permute-start.4 = (bf16[64,128]{1,0:T(8,128)(2,1)S(1)}, bf16[64,128]{1,0:T(8,128)(2,1)S(1)}, u32[]{:S(2)}, u32[]{:S(2)}) collective-permute-start(bf16[64,128]{1,0:T(8,128)(2,1)S(1)} %get-tuple-element.55), channel_id=1, source_target_pairs={{0,8},{8,0},{16,24},{24,16},{1,9},{9,1},{17,25},{25,17},{2,10},{10... | collective-permute-start | bytes 49160 | tf_op jit(solution)/shard_map/ppermute | solution.py:20
  88.0 0.2 collective-permute-start.5
  88.2 3.0 %collective-permute-done.3.row_ref = bf16[64,128]{1,0:T(8,128)(2,1)S(1)} collective-permute-done((bf16[64,128]{1,0:T(8,128)(2,1)S(1)}, bf16[64,128]{1,0:T(8,128)(2,1)S(1)}, u32[]{:S(2)}, u32[]{:S(2)}) %collective-permute-start.3) | collective-permute-done | bytes 16416 | tf_op jit(solution)/shard_map/ppermute | solution.py:20
  91.1 0.0 collective-permute-done.4.col_ref
  91.1 2.4 %collective-permute-done.5.corner_ref = bf16[64,128]{1,0:T(8,128)(2,1)S(1)} collective-permute-done((bf16[64,128]{1,0:T(8,128)(2,1)S(1)}, bf16[64,128]{1,0:T(8,128)(2,1)S(1)}, u32[]{:S(2)}, u32[]{:S(2)}) %collective-permute-start.5) | collective-permute-done | bytes 16416 | tf_op jit(solution)/shard_map/ppermute | solution.py:20
  93.5 0.0 copy-done.13
  93.5 3.2 %shard_map.142 = bf16[40,64,128]{2,1,0:T(8,128)(2,1)S(1)} custom-call(bf16[40,64,128]{2,1,0:T(8,128)(2,1)S(1)} %get-tuple-element.53.d_ref.da_ref, bf16[64,128]{1,0:T(8,128)(2,1)S(1)} %collective-permute-done.3.row_ref, bf16[64,128]{1,0:T(8,128)(2,1)S(1)} %collective-permute-done.4.col_ref, bf16[64,128]{1,0:T(8,128)(2,1)S(1)} %collective-permute-done.5.corner_ref, ...), custom_call_target="tpu_custom_call" | custom-call | tf_op jit(solution)/shard_map/pallas_call | solution.py:556
  96.8 1.3 %copy.15 = bf16[1,1,64,40,128]{4,3,2,1,0:T(8,128)(2,1)} copy(bf16[1,1,64,40,128]{4,2,3,1,0:T(8,128)(2,1)S(1)} %bitcast.16) | data formatting | bytes 1310720
  98.0 0.0 all-to-all-done.4
  98.0 0.8 shard_map.145
  (19 shorter events, 0.0 us)
Async XLA Ops:
  0.6 1.1 %copy-start.7 = (bf16[1,1,64,40,128]{4,3,2,1,0:T(8,128)(2,1)S(1)}, bf16[1,1,64,40,128]{4,3,2,1,0:T(8,128)(2,1)}, u32[]{:S(2)}) copy-start(bf16[1,1,64,40,128]{4,3,2,1,0:T(8,128)(2,1)} %param.8) | copy-start | bytes 1966084
  3.1 8.8 %collective-permute-start = (bf16[64,128]{1,0:T(8,128)(2,1)S(1)}, bf16[64,128]{1,0:T(8,128)(2,1)S(1)}, u32[]{:S(2)}, u32[]{:S(2)}) collective-permute-start(bf16[64,128]{1,0:T(8,128)(2,1)S(1)} %get-tuple-element.38), channel_id=1, source_target_pairs={{0,16},{8,24},{16,0},{24,8},{1,17},{9,25},{17,1},{25,9},{2,18},{10... | collective-permute-start | bytes 49160 | tf_op jit(solution)/shard_map/ppermute | solution.py:20
  7.1 4.8 %collective-permute-start.1 = (bf16[64,128]{1,0:T(8,128)(2,1)S(1)}, bf16[64,128]{1,0:T(8,128)(2,1)S(1)}, u32[]{:S(2)}, u32[]{:S(2)}) collective-permute-start(bf16[64,128]{1,0:T(8,128)(2,1)S(1)} %get-tuple-element.39), channel_id=1, source_target_pairs={{0,8},{8,0},{16,24},{24,16},{1,9},{9,1},{17,25},{25,17},{2,10},{10... | collective-permute-start | bytes 49160 | tf_op jit(solution)/shard_map/ppermute | solution.py:20
  8.7 5.5 %collective-permute-start.2 = (bf16[64,128]{1,0:T(8,128)(2,1)S(1)}, bf16[64,128]{1,0:T(8,128)(2,1)S(1)}, u32[]{:S(2)}, u32[]{:S(2)}) collective-permute-start(bf16[64,128]{1,0:T(8,128)(2,1)S(1)} %get-tuple-element.40), channel_id=1, source_target_pairs={{0,24},{8,16},{16,8},{24,0},{1,25},{9,17},{17,9},{25,1},{2,26},{10... | collective-permute-start | bytes 49160 | tf_op jit(solution)/shard_map/ppermute | solution.py:20
  8.7 0.8 copy-start.8
  9.5 0.9 copy-start.11
  10.6 0.6 copy-start.12
  11.2 0.6 copy-start.14
  17.8 1.4 %copy-start.3 = (bf16[42,192,128]{2,1,0:T(8,128)(2,1)}, bf16[42,192,128]{2,1,0:T(8,128)(2,1)S(1)}, u32[]{:S(2)}) copy-start(bf16[42,192,128]{2,1,0:T(8,128)(2,1)S(1)} %get-tuple-element.58.shifted_ref) | copy-start | bytes 6193156
  29.3 0.8 copy-start.9
  30.1 0.7 copy-start.21
  30.7 0.7 copy-start.23
  34.4 1.1 %copy-start = (f32[40,64,128]{2,1,0:T(8,128)}, f32[40,64,128]{2,1,0:T(8,128)S(1)}, u32[]{:S(2)}) copy-start(f32[40,64,128]{2,1,0:T(8,128)S(1)} %get-tuple-element.42.a_ref) | copy-start | bytes 3932164
  35.5 1.0 %copy-start.5 = (bf16[40,128,128]{2,1,0:T(8,128)(2,1)}, bf16[40,128,128]{2,1,0:T(8,128)(2,1)S(1)}, u32[]{:S(2)}) copy-start(bf16[40,128,128]{2,1,0:T(8,128)(2,1)S(1)} %get-tuple-element.45.turn_ref) | copy-start | bytes 3932164
  36.5 0.6 copy-start.16
  37.2 0.6 copy-start.18
  37.8 11.1 %all-to-all-start.1 = ((bf16[8,96,128]{2,1,0:T(8,128)(2,1)}), bf16[8,96,128]{2,1,0:T(8,128)(2,1)S(1)}, u32[]{:S(2)}, u32[]{:S(2)}) async-start(bf16[8,96,128]{2,1,0:T(8,128)(2,1)} %get-tuple-element.46), calls=%async_computation.1 | async-start | bytes 393216 | tf_op jit(solution)/shard_map/all_to_all | solution.py:569
  41.2 1.7 %copy-start.2 = (bf16[1,1,256,40,128]{4,3,2,1,0:T(8,128)(2,1)S(1)}, bf16[1,1,256,40,128]{4,3,2,1,0:T(8,128)(2,1)}, u32[]{:S(2)}) copy-start(bf16[1,1,256,40,128]{4,3,2,1,0:T(8,128)(2,1)} %param.9) | copy-start | bytes 7864324
  42.9 6.0 %copy-start.10 = (bf16[64,256]{1,0:T(8,128)(2,1)S(1)}, bf16[64,256]{1,0:T(8,128)(2,1)}, u32[]{:S(2)}) copy-start(bf16[64,256]{1,0:T(8,128)(2,1)} %wt_ref.3) | copy-start | bytes 98308
  42.9 6.0 %copy-start.20 = (f32[256]{0:T(256)S(1)}, f32[256]{0:T(256)}, u32[]{:S(2)}) copy-start(f32[256]{0:T(256)} %param.14) | copy-start | bytes 3076
  42.9 6.0 %copy-start.25 = (f32[256]{0:T(256)S(1)}, f32[256]{0:T(256)}, u32[]{:S(2)}) copy-start(f32[256]{0:T(256)} %param.15) | copy-start | bytes 3076
  48.9 1.3 %copy-start.6 = (bf16[40,128,128]{2,1,0:T(8,128)(2,1)S(1)}, bf16[40,128,128]{2,1,0:T(8,128)(2,1)}, u32[]{:S(2)}) copy-start(bf16[40,128,128]{2,1,0:T(8,128)(2,1)} %copy-done.5) | copy-start | bytes 3932164
  50.2 0.8 copy-start.15
  51.1 15.7 %copy-start.1 = (f32[40,64,128]{2,1,0:T(8,128)S(1)}, f32[40,64,128]{2,1,0:T(8,128)}, u32[]{:S(2)}) copy-start(f32[40,64,128]{2,1,0:T(8,128)} %copy-done) | copy-start | bytes 3932164
  51.1 15.7 %copy-start.17 = (f32[64,256]{1,0:T(8,128)S(1)}, f32[64,256]{1,0:T(8,128)}, u32[]{:S(2)}) copy-start(f32[64,256]{1,0:T(8,128)} %copy-done.16) | copy-start | bytes 196612
  51.1 15.7 %copy-start.19 = (f32[64,128]{1,0:T(8,128)S(1)}, f32[64,128]{1,0:T(8,128)}, u32[]{:S(2)}) copy-start(f32[64,128]{1,0:T(8,128)} %copy-done.18) | copy-start | bytes 98308
  51.1 15.7 %copy-start.22 = (f32[64]{0:T(128)S(1)}, f32[64]{0:T(128)}, u32[]{:S(2)}) copy-start(f32[64]{0:T(128)} %param.12) | copy-start | bytes 772
  51.1 15.7 %copy-start.24 = (f32[64]{0:T(128)S(1)}, f32[64]{0:T(128)}, u32[]{:S(2)}) copy-start(f32[64]{0:T(128)} %param.13) | copy-start | bytes 772
  57.6 12.0 %copy-start.4 = (bf16[42,192,128]{2,1,0:T(8,128)(2,1)S(1)}, bf16[42,192,128]{2,1,0:T(8,128)(2,1)}, u32[]{:S(2)}) copy-start(bf16[42,192,128]{2,1,0:T(8,128)(2,1)} %copy-done.3) | copy-start | bytes 6193156
  69.6 24.0 %copy-start.13 = (bf16[64,576]{1,0:T(8,128)(2,1)S(1)}, bf16[64,576]{1,0:T(8,128)(2,1)}, u32[]{:S(2)}) copy-start(bf16[64,576]{1,0:T(8,128)(2,1)} %copy-done.12) | copy-start | bytes 221188
  81.1 16.9 %all-to-all-start.4 = ((bf16[32,16,128]{2,1,0:T(8,128)(2,1)}), bf16[32,16,128]{2,1,0:T(8,128)(2,1)S(1)}, u32[]{:S(2)}, u32[]{:S(2)}) async-start(bf16[32,16,128]{2,1,0:T(8,128)(2,1)} %shard_map.144), calls=%async_computation.4 | async-start | bytes 262144 | tf_op jit(solution)/shard_map/all_to_all | solution.py:569
  83.7 7.4 %collective-permute-start.3 = (bf16[64,128]{1,0:T(8,128)(2,1)S(1)}, bf16[64,128]{1,0:T(8,128)(2,1)S(1)}, u32[]{:S(2)}, u32[]{:S(2)}) collective-permute-start(bf16[64,128]{1,0:T(8,128)(2,1)S(1)} %get-tuple-element.54), channel_id=1, source_target_pairs={{0,16},{8,24},{16,0},{24,8},{1,17},{9,25},{17,1},{25,9},{2,18},{10... | collective-permute-start | bytes 49160 | tf_op jit(solution)/shard_map/ppermute | solution.py:20
  86.4 4.7 %collective-permute-start.4 = (bf16[64,128]{1,0:T(8,128)(2,1)S(1)}, bf16[64,128]{1,0:T(8,128)(2,1)S(1)}, u32[]{:S(2)}, u32[]{:S(2)}) collective-permute-start(bf16[64,128]{1,0:T(8,128)(2,1)S(1)} %get-tuple-element.55), channel_id=1, source_target_pairs={{0,8},{8,0},{16,24},{24,16},{1,9},{9,1},{17,25},{25,17},{2,10},{10... | collective-permute-start | bytes 49160 | tf_op jit(solution)/shard_map/ppermute | solution.py:20
  88.0 5.5 %collective-permute-start.5 = (bf16[64,128]{1,0:T(8,128)(2,1)S(1)}, bf16[64,128]{1,0:T(8,128)(2,1)S(1)}, u32[]{:S(2)}, u32[]{:S(2)}) collective-permute-start(bf16[64,128]{1,0:T(8,128)(2,1)S(1)} %get-tuple-element.56), channel_id=1, source_target_pairs={{0,24},{8,16},{16,8},{24,0},{1,25},{9,17},{17,9},{25,1},{2,26},{10... | collective-permute-start | bytes 49160 | tf_op jit(solution)/shard_map/ppermute | solution.py:20

commit v2 on v1

--- a/solution.py
+++ b/solution.py
@@ -30,11 +30,6 @@
 
 def lane_pair(ref, row):
     return jnp.concatenate([ref[row], ref[row + 1]], axis=1)
-
-
-def fold_pair(value):
-    half = value.shape[1] // 2
-    return value[:, :half] + value[:, half:]
 
 
 def row_of(partials):
@@ -117,7 +112,7 @@
 
     kind = row_ref.dtype
     block = pl.ds(at, depth)
-    found = lax.fori_loop(0, rows, body, jnp.zeros((depth, cols), f32), unroll=4)
+    found = lax.fori_loop(0, rows, body, jnp.zeros((depth, cols), f32), unroll=rows)
     col_ref[block] = found.astype(kind)
     border = line_of(jnp.where(half == 0, rows - 1, 0))
     row_ref[block] = border.astype(kind)
@@ -131,16 +126,14 @@
     depth, cols = border.shape
     column, half = place_flags()
     lane = lax.broadcasted_iota(jnp.int32, (depth, cols), 1)
-    left = jnp.where(column == 1, side, 0.0)
-    right = jnp.where(column == 0, side, 0.0)
+    start = jnp.where(column == 1, cols, 2 * cols - 1)
 
     def place(r, line):
         before = pltpu.roll(line, 1, 1)
         after = pltpu.roll(line, cols - 1, 1)
-        edge_left = pltpu.roll(left, (cols - r) % cols, 1)
-        edge_right = pltpu.roll(right, (2 * cols - 1 - r) % cols, 1)
-        before = jnp.where(lane == 0, edge_left, before)
-        after = jnp.where(lane == cols - 1, edge_right, after)
+        edge = pltpu.roll(side, lax.rem(start - r, cols), 1)
+        before = jnp.where(lane == 0, jnp.where(column == 1, edge, 0.0), before)
+        after = jnp.where(lane == cols - 1, jnp.where(column == 0, edge, 0.0), after)
         out_ref[r] = jnp.concatenate([before, line, after], axis=0).astype(bf16)
 
     place(0, jnp.where(half == 1, border, 0.0))
@@ -150,15 +143,21 @@
         place(h + 1, line_of(h))
         return carry
 
-    lax.fori_loop(0, rows, body, 0, unroll=4)
-
-
-def conv_pair(weights, shifted_ref, row):
+    lax.fori_loop(0, rows, body, 0, unroll=rows)
+
+
+def conv_lines(weights, shifted_ref, row):
     depth3 = shifted_ref.shape[1]
     cols = shifted_ref.shape[2]
-    first = shifted_ref[pl.ds(row, 3)].reshape(3 * depth3, cols)
-    second = shifted_ref[pl.ds(row + 1, 3)].reshape(3 * depth3, cols)
-    return nn_dot(weights, jnp.concatenate([first, second], axis=1))
+    depth = depth3 // 3
+    first = shifted_ref[pl.ds(row, 4)].reshape(4 * depth3, cols)
+    second = shifted_ref[pl.ds(row + 2, 4)].reshape(4 * depth3, cols)
+    found = nn_dot(weights, jnp.concatenate([first, second], axis=1))
+    return [
+        found[u * depth : (u + 1) * depth, k * cols : (k + 1) * cols]
+        for k in range(2)
+        for u in range(2)
+    ]
 
 
 def to_lines(planes_ref, out_ref, tall_ref):
@@ -178,7 +177,7 @@
             out_ref[h, start : start + block] = line.astype(bf16)
             return carry
 
-        lax.fori_loop(0, rows, collect, 0, unroll=4)
+        lax.fori_loop(0, rows, collect, 0, unroll=rows)
 
 
 def edge_kernel(planes_ref, lines_ref, row_ref, col_ref, corner_ref, tall_ref):
@@ -208,8 +207,10 @@
         for b in range(3):
             forth.append(conv_ref[a, b])
             back.append(turned(conv_ref[2 - a, 2 - b].astype(f32)).astype(bf16))
-    ahead_ref[...] = jnp.concatenate(forth, axis=1)
-    behind_ref[...] = jnp.concatenate(back, axis=1)
+    gap = [jnp.zeros((depth, depth), bf16)] * 3
+    for ref, blocks in ((ahead_ref, forth), (behind_ref, back)):
+        ref[:depth] = jnp.concatenate(blocks + gap, axis=1)
+        ref[depth:] = jnp.concatenate(gap + blocks, axis=1)
     for k in range(0, wide, 128):
         block = proj_ref[:, k : k + 128].astype(f32)
         block = jnp.concatenate([block, jnp.zeros((128 - depth, 128), f32)], axis=0)
@@ -223,20 +224,20 @@
     weights = w_ref[...]
 
     def body(j, total):
-        h = 2 * j
-        both = conv_pair(weights, shifted_ref, h)
-        a_ref[h] = both[:, :cols]
-        a_ref[h + 1] = both[:, cols:]
-        return total + fold_pair(both)
-
-    total = lax.fori_loop(0, rows // 2, body, jnp.zeros((depth, cols), f32), unroll=4)
+        h = 4 * j
+        for k, line in enumerate(conv_lines(weights, shifted_ref, h)):
+            a_ref[h + k] = line
+            total = total + line
+        return total
+
+    total = lax.fori_loop(0, rows // 4, body, jnp.zeros((depth, cols), f32), unroll=rows // 4)
     mean = jnp.sum(total, axis=1, keepdims=True) * (1.0 / (rows * cols))
 
     def spread(h, squares):
         centred = a_ref[h] - mean
         return squares + centred * centred
 
-    squares = lax.fori_loop(0, rows, spread, jnp.zeros((depth, cols), f32), unroll=4)
+    squares = lax.fori_loop(0, rows, spread, jnp.zeros((depth, cols), f32), unroll=rows)
     pack_rows(stat_ref, [row_of(total) * (1.0 / (rows * cols)), row_of(squares)])
 
 
@@ -288,7 +289,7 @@
 
     zero = jnp.zeros((depth, cols), f32)
     both = jnp.zeros((2 * depth, cols), f32)
-    total, turned = lax.fori_loop(0, rows, activate, (zero, both), unroll=4)
+    total, turned = lax.fori_loop(0, rows, activate, (zero, both), unroll=rows)
     gram = jnp.zeros((depth, 3 * depth), f32)
     step = 8
     for h in range(0, rows, step):
@@ -331,24 +332,24 @@
     wide = w_ref.shape[0]
     mean, scale, gain, shift = norm_columns(stat_ref, gain_ref, shift_ref, float(rows * cols))
     steep = 0.5 * gain * scale
-    keep_ref[0] = spread_column(mean, cols)
-    keep_ref[1] = spread_column(steep, cols)
-    keep_ref[2] = spread_column(0.5 * shift, cols)
+    keep_ref[0] = spread_column(steep, cols)
+    keep_ref[1] = spread_column(0.5 * shift - mean * steep, cols)
+    keep_ref[2] = jnp.zeros((wide, cols), f32)
     keep_ref[3] = jnp.zeros((wide, cols), f32)
-    keep_ref[4] = jnp.zeros((wide, cols), f32)
-    block = 128
+    proj_ref[...] = jnp.zeros(proj_ref.shape, f32)
+    block = 64
     weights_t = wt_ref[...]
 
-    def body(j, carry):
+    def expand(j):
         h = 2 * j
         lines = lane_pair(y_ref, h)
         for start in range(0, wide, block):
             part = slice(start, start + block)
             both = nn_dot(w_ref[part], lines)
-            m, s, b = keep_ref[0, part], keep_ref[1, part], keep_ref[2, part]
+            s, b = keep_ref[0, part], keep_ref[1, part]
             total = cross = None
             for k in range(2):
-                half = (both[:, k * cols : (k + 1) * cols] - m) * s + b
+                half = both[:, k * cols : (k + 1) * cols] * s + b
                 t = jnp.tanh(half)
                 slope = (1.0 + t) * (1.0 + half * (1.0 - t))
                 grad = g_ref[h + k, part].astype(f32) * slope
@@ -356,33 +357,31 @@
                 across = grad * half
                 total = grad if total is None else total + grad
                 cross = across if cross is None else cross + across
-            keep_ref[3, part] += total
-            keep_ref[4, part] += cross
-        return carry
-
-    lax.fori_loop(0, rows // 2, body, 0, unroll=2)
-
-    depth2 = 2 * depth
+            keep_ref[2, part] += total
+            keep_ref[3, part] += cross
 
     def narrow(j, turned):
         h = 2 * j
-        both = nn_dot(weights_t, lane_pair(e_ref, h))
+        scaled = lane_pair(e_ref, h)
+        both = nn_dot(weights_t, scaled)
+        proj_ref[...] += nt_dot(lane_pair(y_ref, h), scaled)
         for k in range(2):
             line = both[:, k * cols : (k + 1) * cols]
             f_ref[h + k] = line
             turned = turned + jnp.concatenate([line, line], axis=0) * turn_ref[h + k].astype(f32)
         return turned
 
-    turned = lax.fori_loop(0, rows // 2, narrow, jnp.zeros((depth2, cols), f32), unroll=4)
-    proj_ref[...] = jnp.zeros(proj_ref.shape, f32)
-    step = 8
-    for start in range(0, rows, step):
-        lines = range(start, min(start + step, rows))
-        left = jnp.concatenate([y_ref[h] for h in lines], axis=1)
-        right = jnp.concatenate([e_ref[h] for h in lines], axis=1)
-        proj_ref[...] += nt_dot(left, right)
-    total = row_of(keep_ref[3]) * 0.5
-    cross = row_of(keep_ref[4])
+    def body(j, turned):
+        expand(j)
+        turned = narrow(j - 1, turned)
+        return turned
+
+    expand(0)
+    turned = jnp.zeros((2 * depth, cols), f32)
+    turned = lax.fori_loop(1, rows // 2, body, turned, unroll=rows // 2 - 1)
+    turned = narrow(rows // 2 - 1, turned)
+    total = row_of(keep_ref[2]) * 0.5
+    cross = row_of(keep_ref[3])
     cross = (cross - shift_ref[...] * total) / gain_ref[...]
     pack_rows(out_ref, [total, cross, row_of(turned)])
 
@@ -455,7 +454,7 @@
             da_ref[h + k] = (back_front * (grad - flat - normed * tilt)).astype(bf16)
         return carry
 
-    lax.fori_loop(0, rows // 2, narrow, 0, unroll=4)
+    lax.fori_loop(0, rows // 2, narrow, 0, unroll=rows // 2)
     edge_pieces(
         lambda h: da_ref[h].astype(f32), rows, (depth, cols), row_ref, col_ref, corner_ref
     )
@@ -471,7 +470,7 @@
         padded_ref[h + 2] = da_ref[h]
         return carry
 
-    lax.fori_loop(0, rows, fill, 0, unroll=8)
+    lax.fori_loop(0, rows, fill, 0, unroll=rows)
     tall = 3 * depth
     step = 6
     grad = jnp.zeros((tall, tall), f32)
@@ -496,20 +495,24 @@
     out_ref[at:] = jnp.zeros((out_ref.shape[0] - at, 128), bf16)
 
 
-def back_kernel(d_ref, row_ref, col_ref, corner_ref, w_ref, out_ref, shifted_ref):
-    rows, _, cols = d_ref.shape
-    side = col_ref[...].astype(f32) + corner_ref[...].astype(f32)
-    three_shifts(lambda h: d_ref[h].astype(f32), row_ref[...].astype(f32), side, shifted_ref)
+def beside_kernel(row_ref, col_ref, corner_ref, out_ref):
+    out_ref[0] = row_ref[...]
+    out_ref[1] = col_ref[...] + corner_ref[...]
+
+
+def back_kernel(d_ref, beside_ref, w_ref, out_ref, shifted_ref):
+    rows, _, _ = d_ref.shape
+    border, side = beside_ref[0].astype(f32), beside_ref[1].astype(f32)
+    three_shifts(lambda h: d_ref[h].astype(f32), border, side, shifted_ref)
     weights = w_ref[...]
 
     def body(j, carry):
-        h = 2 * j
-        both = conv_pair(weights, shifted_ref, h).astype(bf16)
-        out_ref[h] = both[:, :cols]
-        out_ref[h + 1] = both[:, cols:]
+        h = 4 * j
+        for k, line in enumerate(conv_lines(weights, shifted_ref, h)):
+            out_ref[h + k] = line.astype(bf16)
         return carry
 
-    lax.fori_loop(0, rows // 2, body, 0, unroll=4)
+    lax.fori_loop(0, rows // 4, body, 0, unroll=rows // 4)
 
 
 def sum_kernel(parts_ref, out_ref):
@@ -584,7 +587,7 @@
     rows_out = ((group, 8, 128), f32)
 
     tall = pltpu.VMEM((depth * rows, cols), f32)
-    keep = [pltpu.VMEM((5, wide, cols), f32)]
+    keep = [pltpu.VMEM((4, wide, cols), f32)]
     lines, *edges = call(
         edge_kernel, EDGE, [(plane, bf16)] + [piece] * 3, images[0, 0], scratch=[tall]
     )
@@ -593,7 +596,7 @@
     )
     ahead, behind, proj_t = call(
         weights_kernel, 4,
-        [((depth, 9 * depth), bf16)] * 2 + [((wide, depth), bf16)], conv_weight, proj_weight,
+        [((2 * depth, 12 * depth), bf16)] * 2 + [((wide, depth), bf16)], conv_weight, proj_weight,
     )
     edges = exchange(*edges)
     triple = pltpu.VMEM((rows + 2, 3 * depth, cols), bf16)
@@ -629,13 +632,15 @@
         corr_kernel, GRAD, [((used, 128), bf16)], grad_conv, shifted, proj, small,
         scratch=[pltpu.VMEM((rows + 4, depth, cols), bf16)],
     )
+    (last,) = call(beside_kernel, 1, [((2, depth, cols), bf16)], *last)
     (grad_field,) = call(
-        back_kernel, BACK, [(plane, bf16)], grad_conv, *last, behind, scratch=[triple]
+        back_kernel, BACK, [(plane, bf16)], grad_conv, last, behind, scratch=[triple]
     )
     part = jnp.pad(part, ((0, -used % (devices * 16)), (0, 0))).reshape(devices, -1, 128)
     parts = swap(part, all_axes)
     (mine,) = call(sum_kernel, 4, [(part.shape, bf16)], parts)
-    full = swap(mine, all_axes).reshape(-1, 128)[:used]
+    full = swap(mine, all_axes)
+    full = full.reshape(-1, 128)[:used]
     kernel_total, proj_total, gain1, shift1, gain3, shift3 = call(
         partial(unpack_kernel, factor=per_image), 4,
         [((3, 3, depth, depth), f32), ((depth, wide), f32)]

time: 99.6 us -> 90.3 us (0.907)
  Pallas kernels: 24.5 us -> 14.9 us
    pallas_call x11 -> x12, Pallas kernels: 24.5 us -> 14.9 us  [call(): pl.pallas_call(kernel, out_shape=[jax.ShapeDtypeStruct(s, d) for s, d in...]
  transfers between devices with their start and end apart: 8 -> 8, of which waited for: 4 -> 4; matrix products, arithmetic and copies ran while one was open for 1% -> 1% of each run, Pallas kernels for 5% -> 3%
where the time goes in v2:
time: 90.3 us; the launch traced here: 89.6 us
  blocking collectives  29.4 us (33%)
  starting transfers between devices  16.1 us (18%)
  local copies, waits for them, and re-layouts  16 us (18%)
  Pallas kernels  14.9 us (17%)
  waiting for transfers between devices  12.3 us (14%)
    all_to_all x3, blocking collectives, swap(): return lax.all_to_all(copies, axes, 0, 0)  29.4 us
    unnamed x53, local copies, waits for them, and re-layouts  16 us
    pallas_call x12, Pallas kernels, call(): pl.pallas_call(kernel, out_shape=[jax.ShapeDtypeStruct(s, d) for s, d in...  14.9 us
    ppermute x6, starting transfers between devices, from_partner(): lax.ppermute(value, 'sp', [(i, i ^ mask) for i in range(lax.axis_size('sp...  10.2 us
    ppermute x6, waiting for transfers between devices, from_partner(): lax.ppermute(value, 'sp', [(i, i ^ mask) for i in range(lax.axis_size('sp...  7.63 us
    all_to_all x2, starting transfers between devices, swap(): return lax.all_to_all(copies, axes, 0, 0)  5.97 us
    all_to_all x2, waiting for transfers between devices, swap(): return lax.all_to_all(copies, axes, 0, 0)  4.69 us
  transfers between devices with their start and end apart: 8, of which 4 were waited for; matrix products, arithmetic and copies ran while one was open for 1% of the time, Pallas kernels for 3%

profile of v2, /device:TPU:0, one launch (start us, length us, event | category | flops | bytes accessed | tf_op | source)
XLA Modules:
  0.0 89.6 jit_solution(15690418600508026177)
XLA Ops:
  0.6 0.0 copy-start.7
  0.6 1.1 %copy-done.7 = bf16[1,1,64,40,128]{4,3,2,1,0:T(8,128)(2,1)S(1)} copy-done((bf16[1,1,64,40,128]{4,3,2,1,0:T(8,128)(2,1)S(1)}, bf16[1,1,64,40,128]{4,3,2,1,0:T(8,128)(2,1)}, u32[]{:S(2)}) %copy-start.7) | copy-done | bytes 655384
  1.7 0.4 shard_map.135
  2.1 4.1 %collective-permute-start = (bf16[64,128]{1,0:T(8,128)(2,1)S(1)}, bf16[64,128]{1,0:T(8,128)(2,1)S(1)}, u32[]{:S(2)}, u32[]{:S(2)}) collective-permute-start(bf16[64,128]{1,0:T(8,128)(2,1)S(1)} %get-tuple-element.38), channel_id=1, source_target_pairs={{0,16},{8,24},{16,0},{24,8},{1,17},{9,25},{17,1},{25,9},{2,18},{10... | collective-permute-start | bytes 49160 | tf_op jit(solution)/shard_map/ppermute | solution.py:20
  6.3 1.6 %collective-permute-start.1 = (bf16[64,128]{1,0:T(8,128)(2,1)S(1)}, bf16[64,128]{1,0:T(8,128)(2,1)S(1)}, u32[]{:S(2)}, u32[]{:S(2)}) collective-permute-start(bf16[64,128]{1,0:T(8,128)(2,1)S(1)} %get-tuple-element.39), channel_id=1, source_target_pairs={{0,8},{8,0},{16,24},{24,16},{1,9},{9,1},{17,25},{25,17},{2,10},{10... | collective-permute-start | bytes 49160 | tf_op jit(solution)/shard_map/ppermute | solution.py:20
  7.8 0.0 collective-permute-start.2
  7.8 0.8 copy-done.8
  8.6 0.9 %copy-done.13 = bf16[3,3,64,64]{3,2,1,0:T(8,128)(2,1)S(1)} copy-done((bf16[3,3,64,64]{3,2,1,0:T(8,128)(2,1)S(1)}, bf16[3,3,64,64]{3,2,1,0:T(8,128)(2,1)}, u32[]{:S(2)}) %copy-start.13) | copy-done | bytes 73752
  9.5 0.3 shard_map.136
  9.8 0.0 copy-start.11
  9.8 0.7 copy-done.11
  10.4 0.6 copy-done.14
  11.1 0.0 collective-permute-done.row_ref
  11.1 0.0 collective-permute-done.1.col_ref
  11.1 2.3 %collective-permute-done.2.corner_ref = bf16[64,128]{1,0:T(8,128)(2,1)S(1)} collective-permute-done((bf16[64,128]{1,0:T(8,128)(2,1)S(1)}, bf16[64,128]{1,0:T(8,128)(2,1)S(1)}, u32[]{:S(2)}, u32[]{:S(2)}) %collective-permute-start.2) | collective-permute-done | bytes 16416 | tf_op jit(solution)/shard_map/ppermute | solution.py:20
  13.4 1.2 %shard_map.137 = (bf16[42,192,128]{2,1,0:T(8,128)(2,1)S(1)}, f32[40,64,128]{2,1,0:T(8,128)S(1)}, f32[8,8,128]{2,1,0:T(8,128)S(1)}) custom-call(bf16[40,64,128]{2,1,0:T(8,128)(2,1)S(1)} %get-tuple-element.37.x_ref, bf16[64,128]{1,0:T(8,128)(2,1)S(1)} %collective-permute-done.row_ref, bf16[64,128]{1,0:T(8,128)(2,1)S(1)} %collective-permute-done.1.col_ref, ...), custom_call_target="tpu_custom_call" | custom-call | tf_op jit(solution)/shard_map/pallas_call | solution.py:559
  14.6 0.0 copy-start.3
  14.6 1.3 %copy-done.3 = bf16[42,192,128]{2,1,0:T(8,128)(2,1)} copy-done((bf16[42,192,128]{2,1,0:T(8,128)(2,1)}, bf16[42,192,128]{2,1,0:T(8,128)(2,1)S(1)}, u32[]{:S(2)}) %copy-start.3) | copy-done | bytes 2064408
  16.0 10.2 %all_to_all.25.stat_ref.stat1_ref = f32[8,8,128]{2,1,0:T(8,128)S(1)} all-to-all(f32[8,8,128]{2,1,0:T(8,128)S(1)} %get-tuple-element.43), channel_id=1, replica_groups=mesh['sp'=4,'bn'=2,'dp'=4] {'sp','bn'}, dimensions={0} | all-to-all | bytes 65536 | tf_op jit(solution)/shard_map/all_to_all | solution.py:572
  26.2 0.8 copy-done.9
  26.9 0.7 copy-done.21
  27.6 0.7 copy-done.23
  28.2 2.9 %shard_map.138 = (bf16[40,64,128]{2,1,0:T(8,128)(2,1)S(1)}, bf16[40,128,128]{2,1,0:T(8,128)(2,1)S(1)}, bf16[8,96,128]{2,1,0:T(8,128)(2,1)}, f32[64,256]{1,0:T(8,128)S(1)}, f32[64,128]{1,0:T(8,128)S(1)}) custom-call(f32[40,64,128]{2,1,0:T(8,128)S(1)} %get-tuple-element.42.a_ref, f32[8,8,128]{2,1,0:T(8,128)S(1)} %all_to_all.25.stat_ref.stat1_ref, ...), custom_call_target="tpu_custom_call" | custom-call | tf_op jit(solution)/shard_map/pallas_call | solution.py:559
  31.1 1.1 %copy-done = f32[40,64,128]{2,1,0:T(8,128)} copy-done((f32[40,64,128]{2,1,0:T(8,128)}, f32[40,64,128]{2,1,0:T(8,128)S(1)}, u32[]{:S(2)}) %copy-start) | copy-done | bytes 1310744
  32.2 1.0 %copy-done.5 = bf16[40,128,128]{2,1,0:T(8,128)(2,1)} copy-done((bf16[40,128,128]{2,1,0:T(8,128)(2,1)}, bf16[40,128,128]{2,1,0:T(8,128)(2,1)S(1)}, u32[]{:S(2)}) %copy-start.5) | copy-done | bytes 1310744
  33.2 0.6 copy-done.16
  33.8 0.6 copy-done.18
  34.4 3.4 %all-to-all-start.1 = ((bf16[8,96,128]{2,1,0:T(8,128)(2,1)}), bf16[8,96,128]{2,1,0:T(8,128)(2,1)S(1)}, u32[]{:S(2)}, u32[]{:S(2)}) async-start(bf16[8,96,128]{2,1,0:T(8,128)(2,1)} %get-tuple-element.46), calls=%async_computation.1 | async-start | bytes 393216 | tf_op jit(solution)/shard_map/all_to_all | solution.py:572
  37.8 0.0 copy-start.2
  37.9 1.7 %copy-done.2 = bf16[1,1,256,40,128]{4,3,2,1,0:T(8,128)(2,1)S(1)} copy-done((bf16[1,1,256,40,128]{4,3,2,1,0:T(8,128)(2,1)S(1)}, bf16[1,1,256,40,128]{4,3,2,1,0:T(8,128)(2,1)}, u32[]{:S(2)}) %copy-start.2) | copy-done | bytes 2621464
  39.6 1.3 %shard_map.139.g_ref = bf16[40,256,128]{2,1,0:T(8,128)(2,1)S(1)} custom-call(bf16[256,40,128]{2,1,0:T(8,128)(2,1)S(1)} %bitcast.15), custom_call_target="tpu_custom_call" | custom-call | tf_op jit(solution)/shard_map/pallas_call | solution.py:559
  40.9 4.7 %all-to-all-done.1.stat_ref.stat3_ref = bf16[8,96,128]{2,1,0:T(8,128)(2,1)S(1)} async-done(((bf16[8,96,128]{2,1,0:T(8,128)(2,1)}), bf16[8,96,128]{2,1,0:T(8,128)(2,1)S(1)}, u32[]{:S(2)}, u32[]{:S(2)}) %all-to-all-start.1) | async-done | bytes 196640 | tf_op jit(solution)/shard_map/all_to_all | solution.py:572
  45.6 0.0 copy-done.10
  45.6 0.0 copy-done.20
  45.6 0.0 copy-done.25
  45.6 0.0 copy-start.6
  45.6 1.3 %copy-done.6 = bf16[40,128,128]{2,1,0:T(8,128)(2,1)S(1)} copy-done((bf16[40,128,128]{2,1,0:T(8,128)(2,1)S(1)}, bf16[40,128,128]{2,1,0:T(8,128)(2,1)}, u32[]{:S(2)}) %copy-start.6) | copy-done | bytes 1310744
  46.9 0.8 copy-done.15
  47.7 0.0 copy-start.24
  47.8 4.2 %shard_map.140 = (f32[40,64,128]{2,1,0:T(8,128)S(1)}, f32[64,256]{1,0:T(8,128)S(1)}, f32[8,8,128]{2,1,0:T(8,128)S(1)}) custom-call(bf16[40,64,128]{2,1,0:T(8,128)(2,1)S(1)} %get-tuple-element.44.y_ref, bf16[40,256,128]{2,1,0:T(8,128)(2,1)S(1)} %shard_map.139.g_ref, bf16[40,128,128]{2,1,0:T(8,128)(2,1)S(1)} %copy-done.6, ...), custom_call_target="tpu_custom_call" | custom-call | tf_op jit(solution)/shard_map/pallas_call | solution.py:559
  51.9 0.0 copy-start.4
  51.9 9.2 %all_to_all.26.sums_ref = f32[8,8,128]{2,1,0:T(8,128)S(1)} all-to-all(f32[8,8,128]{2,1,0:T(8,128)S(1)} %get-tuple-element.49), channel_id=1, replica_groups=mesh['sp'=4,'bn'=2,'dp'=4] {'sp','bn'}, dimensions={0} | all-to-all | bytes 65536 | tf_op jit(solution)/shard_map/all_to_all | solution.py:572
  61.1 0.0 copy-done.1
  61.1 0.0 copy-done.17
  61.2 0.0 copy-done.19
  61.2 0.0 copy-done.22
  61.2 0.0 copy-done.24
  61.2 1.5 %shard_map.141 = (bf16[40,64,128]{2,1,0:T(8,128)(2,1)S(1)}, bf16[64,128]{1,0:T(8,128)(2,1)S(1)}, bf16[64,128]{1,0:T(8,128)(2,1)S(1)}, bf16[64,128]{1,0:T(8,128)(...) custom-call(bf16[40,64,128]{2,1,0:T(8,128)(2,1)S(1)} %get-tuple-element.44.y_ref, ...), custom_call_target="tpu_custom_call" | custom-call | tf_op jit(solution)/shard_map/pallas_call | solution.py:559
  62.7 0.0 copy-start.12
  62.7 0.0 copy-done.4
  62.7 0.8 shard_map.144
  63.5 10.0 %all_to_all.27.parts_ref = bf16[32,16,128]{2,1,0:T(8,128)(2,1)S(1)} all-to-all(bf16[32,16,128]{2,1,0:T(8,128)(2,1)S(1)} %bitcast.18), channel_id=1, replica_groups=mesh['sp'=4,'bn'=2,'dp'=4] {'sp','bn','dp'}, dimensions={0} | all-to-all | bytes 262144 | tf_op jit(solution)/shard_map/all_to_all | solution.py:572
  73.5 0.7 shard_map.145
  74.2 2.6 %all-to-all-start.4 = ((bf16[32,16,128]{2,1,0:T(8,128)(2,1)}), bf16[32,16,128]{2,1,0:T(8,128)(2,1)S(1)}, u32[]{:S(2)}, u32[]{:S(2)}) async-start(bf16[32,16,128]{2,1,0:T(8,128)(2,1)} %shard_map.145), calls=%async_computation.4 | async-start | bytes 262144 | tf_op jit(solution)/shard_map/all_to_all | solution.py:572
  76.8 2.7 %collective-permute-start.3 = (bf16[64,128]{1,0:T(8,128)(2,1)S(1)}, bf16[64,128]{1,0:T(8,128)(2,1)S(1)}, u32[]{:S(2)}, u32[]{:S(2)}) collective-permute-start(bf16[64,128]{1,0:T(8,128)(2,1)S(1)} %get-tuple-element.54), channel_id=1, source_target_pairs={{0,16},{8,24},{16,0},{24,8},{1,17},{9,25},{17,1},{25,9},{2,18},{10... | collective-permute-start | bytes 49160 | tf_op jit(solution)/shard_map/ppermute | solution.py:20
  79.5 1.5 %collective-permute-start.4 = (bf16[64,128]{1,0:T(8,128)(2,1)S(1)}, bf16[64,128]{1,0:T(8,128)(2,1)S(1)}, u32[]{:S(2)}, u32[]{:S(2)}) collective-permute-start(bf16[64,128]{1,0:T(8,128)(2,1)S(1)} %get-tuple-element.55), channel_id=1, source_target_pairs={{0,8},{8,0},{16,24},{24,16},{1,9},{9,1},{17,25},{25,17},{2,10},{10... | collective-permute-start | bytes 49160 | tf_op jit(solution)/shard_map/ppermute | solution.py:20
  81.0 0.2 collective-permute-start.5
  81.2 3.0 %collective-permute-done.3.row_ref = bf16[64,128]{1,0:T(8,128)(2,1)S(1)} collective-permute-done((bf16[64,128]{1,0:T(8,128)(2,1)S(1)}, bf16[64,128]{1,0:T(8,128)(2,1)S(1)}, u32[]{:S(2)}, u32[]{:S(2)}) %collective-permute-start.3) | collective-permute-done | bytes 16416 | tf_op jit(solution)/shard_map/ppermute | solution.py:20
  84.2 0.0 collective-permute-done.4.col_ref
  84.2 2.4 %collective-permute-done.5.corner_ref = bf16[64,128]{1,0:T(8,128)(2,1)S(1)} collective-permute-done((bf16[64,128]{1,0:T(8,128)(2,1)S(1)}, bf16[64,128]{1,0:T(8,128)(2,1)S(1)}, u32[]{:S(2)}, u32[]{:S(2)}) %collective-permute-start.5) | collective-permute-done | bytes 16416 | tf_op jit(solution)/shard_map/ppermute | solution.py:20
  86.6 0.9 %shard_map.143 = bf16[40,64,128]{2,1,0:T(8,128)(2,1)S(1)} custom-call(bf16[40,64,128]{2,1,0:T(8,128)(2,1)S(1)} %get-tuple-element.53.d_ref.da_ref, bf16[2,64,128]{2,1,0:T(8,128)(2,1)S(1)} %shard_map.142.beside_ref, bf16[128,768]{1,0:T(8,128)(2,1)S(1)} %copy-done.12), custom_call_target="tpu_custom_call" | custom-call | tf_op jit(solution)/shard_map/pallas_call | solution.py:559
  87.5 1.3 %copy.15 = bf16[1,1,64,40,128]{4,3,2,1,0:T(8,128)(2,1)} copy(bf16[1,1,64,40,128]{4,2,3,1,0:T(8,128)(2,1)S(1)} %bitcast.16) | data formatting | bytes 1310720
  88.8 0.0 all-to-all-done.4
  88.8 0.8 shard_map.146
  (20 shorter events, 0.0 us)
Async XLA Ops:
  0.6 1.1 %copy-start.7 = (bf16[1,1,64,40,128]{4,3,2,1,0:T(8,128)(2,1)S(1)}, bf16[1,1,64,40,128]{4,3,2,1,0:T(8,128)(2,1)}, u32[]{:S(2)}) copy-start(bf16[1,1,64,40,128]{4,3,2,1,0:T(8,128)(2,1)} %param.8) | copy-start | bytes 1966084
  2.1 9.0 %collective-permute-start = (bf16[64,128]{1,0:T(8,128)(2,1)S(1)}, bf16[64,128]{1,0:T(8,128)(2,1)S(1)}, u32[]{:S(2)}, u32[]{:S(2)}) collective-permute-start(bf16[64,128]{1,0:T(8,128)(2,1)S(1)} %get-tuple-element.38), channel_id=1, source_target_pairs={{0,16},{8,24},{16,0},{24,8},{1,17},{9,25},{17,1},{25,9},{2,18},{10... | collective-permute-start | bytes 49160 | tf_op jit(solution)/shard_map/ppermute | solution.py:20
  6.3 4.8 %collective-permute-start.1 = (bf16[64,128]{1,0:T(8,128)(2,1)S(1)}, bf16[64,128]{1,0:T(8,128)(2,1)S(1)}, u32[]{:S(2)}, u32[]{:S(2)}) collective-permute-start(bf16[64,128]{1,0:T(8,128)(2,1)S(1)} %get-tuple-element.39), channel_id=1, source_target_pairs={{0,8},{8,0},{16,24},{24,16},{1,9},{9,1},{17,25},{25,17},{2,10},{10... | collective-permute-start | bytes 49160 | tf_op jit(solution)/shard_map/ppermute | solution.py:20
  7.8 5.5 %collective-permute-start.2 = (bf16[64,128]{1,0:T(8,128)(2,1)S(1)}, bf16[64,128]{1,0:T(8,128)(2,1)S(1)}, u32[]{:S(2)}, u32[]{:S(2)}) collective-permute-start(bf16[64,128]{1,0:T(8,128)(2,1)S(1)} %get-tuple-element.40), channel_id=1, source_target_pairs={{0,24},{8,16},{16,8},{24,0},{1,25},{9,17},{17,9},{25,1},{2,26},{10... | collective-permute-start | bytes 49160 | tf_op jit(solution)/shard_map/ppermute | solution.py:20
  7.8 0.8 copy-start.8
  8.6 0.9 %copy-start.13 = (bf16[3,3,64,64]{3,2,1,0:T(8,128)(2,1)S(1)}, bf16[3,3,64,64]{3,2,1,0:T(8,128)(2,1)}, u32[]{:S(2)}) copy-start(bf16[3,3,64,64]{3,2,1,0:T(8,128)(2,1)} %conv_ref.1) | copy-start | bytes 221188
  9.8 0.7 copy-start.11
  10.4 0.6 copy-start.14
  14.6 1.4 %copy-start.3 = (bf16[42,192,128]{2,1,0:T(8,128)(2,1)}, bf16[42,192,128]{2,1,0:T(8,128)(2,1)S(1)}, u32[]{:S(2)}) copy-start(bf16[42,192,128]{2,1,0:T(8,128)(2,1)S(1)} %get-tuple-element.58.shifted_ref) | copy-start | bytes 6193156
  26.2 0.8 copy-start.9
  26.9 0.7 copy-start.21
  27.6 0.7 copy-start.23
  31.1 1.1 %copy-start = (f32[40,64,128]{2,1,0:T(8,128)}, f32[40,64,128]{2,1,0:T(8,128)S(1)}, u32[]{:S(2)}) copy-start(f32[40,64,128]{2,1,0:T(8,128)S(1)} %get-tuple-element.42.a_ref) | copy-start | bytes 3932164
  32.2 1.0 %copy-start.5 = (bf16[40,128,128]{2,1,0:T(8,128)(2,1)}, bf16[40,128,128]{2,1,0:T(8,128)(2,1)S(1)}, u32[]{:S(2)}) copy-start(bf16[40,128,128]{2,1,0:T(8,128)(2,1)S(1)} %get-tuple-element.45.turn_ref) | copy-start | bytes 3932164
  33.2 0.6 copy-start.16
  33.8 0.6 copy-start.18
  34.4 11.1 %all-to-all-start.1 = ((bf16[8,96,128]{2,1,0:T(8,128)(2,1)}), bf16[8,96,128]{2,1,0:T(8,128)(2,1)S(1)}, u32[]{:S(2)}, u32[]{:S(2)}) async-start(bf16[8,96,128]{2,1,0:T(8,128)(2,1)} %get-tuple-element.46), calls=%async_computation.1 | async-start | bytes 393216 | tf_op jit(solution)/shard_map/all_to_all | solution.py:572
  37.8 1.7 %copy-start.2 = (bf16[1,1,256,40,128]{4,3,2,1,0:T(8,128)(2,1)S(1)}, bf16[1,1,256,40,128]{4,3,2,1,0:T(8,128)(2,1)}, u32[]{:S(2)}) copy-start(bf16[1,1,256,40,128]{4,3,2,1,0:T(8,128)(2,1)} %param.9) | copy-start | bytes 7864324
  39.6 6.0 %copy-start.10 = (bf16[64,256]{1,0:T(8,128)(2,1)S(1)}, bf16[64,256]{1,0:T(8,128)(2,1)}, u32[]{:S(2)}) copy-start(bf16[64,256]{1,0:T(8,128)(2,1)} %wt_ref.3) | copy-start | bytes 98308
  39.6 6.0 %copy-start.20 = (f32[256]{0:T(256)S(1)}, f32[256]{0:T(256)}, u32[]{:S(2)}) copy-start(f32[256]{0:T(256)} %param.14) | copy-start | bytes 3076
  39.6 6.0 %copy-start.25 = (f32[256]{0:T(256)S(1)}, f32[256]{0:T(256)}, u32[]{:S(2)}) copy-start(f32[256]{0:T(256)} %param.15) | copy-start | bytes 3076
  45.6 1.3 %copy-start.6 = (bf16[40,128,128]{2,1,0:T(8,128)(2,1)S(1)}, bf16[40,128,128]{2,1,0:T(8,128)(2,1)}, u32[]{:S(2)}) copy-start(bf16[40,128,128]{2,1,0:T(8,128)(2,1)} %copy-done.5) | copy-start | bytes 3932164
  46.9 0.8 copy-start.15
  47.7 13.4 %copy-start.1 = (f32[40,64,128]{2,1,0:T(8,128)S(1)}, f32[40,64,128]{2,1,0:T(8,128)}, u32[]{:S(2)}) copy-start(f32[40,64,128]{2,1,0:T(8,128)} %copy-done) | copy-start | bytes 3932164
  47.7 13.4 %copy-start.17 = (f32[64,256]{1,0:T(8,128)S(1)}, f32[64,256]{1,0:T(8,128)}, u32[]{:S(2)}) copy-start(f32[64,256]{1,0:T(8,128)} %copy-done.16) | copy-start | bytes 196612
  47.7 13.4 %copy-start.19 = (f32[64,128]{1,0:T(8,128)S(1)}, f32[64,128]{1,0:T(8,128)}, u32[]{:S(2)}) copy-start(f32[64,128]{1,0:T(8,128)} %copy-done.18) | copy-start | bytes 98308
  47.7 13.4 %copy-start.22 = (f32[64]{0:T(128)S(1)}, f32[64]{0:T(128)}, u32[]{:S(2)}) copy-start(f32[64]{0:T(128)} %param.12) | copy-start | bytes 772
  47.7 13.4 %copy-start.24 = (f32[64]{0:T(128)S(1)}, f32[64]{0:T(128)}, u32[]{:S(2)}) copy-start(f32[64]{0:T(128)} %param.13) | copy-start | bytes 772
  51.9 10.8 %copy-start.4 = (bf16[42,192,128]{2,1,0:T(8,128)(2,1)S(1)}, bf16[42,192,128]{2,1,0:T(8,128)(2,1)}, u32[]{:S(2)}) copy-start(bf16[42,192,128]{2,1,0:T(8,128)(2,1)} %copy-done.3) | copy-start | bytes 6193156
  62.7 23.9 %copy-start.12 = (bf16[128,768]{1,0:T(8,128)(2,1)S(1)}, bf16[128,768]{1,0:T(8,128)(2,1)}, u32[]{:S(2)}) copy-start(bf16[128,768]{1,0:T(8,128)(2,1)} %copy-done.11) | copy-start | bytes 589828
  74.2 14.6 %all-to-all-start.4 = ((bf16[32,16,128]{2,1,0:T(8,128)(2,1)}), bf16[32,16,128]{2,1,0:T(8,128)(2,1)S(1)}, u32[]{:S(2)}, u32[]{:S(2)}) async-start(bf16[32,16,128]{2,1,0:T(8,128)(2,1)} %shard_map.145), calls=%async_computation.4 | async-start | bytes 262144 | tf_op jit(solution)/shard_map/all_to_all | solution.py:572
  76.8 7.4 %collective-permute-start.3 = (bf16[64,128]{1,0:T(8,128)(2,1)S(1)}, bf16[64,128]{1,0:T(8,128)(2,1)S(1)}, u32[]{:S(2)}, u32[]{:S(2)}) collective-permute-start(bf16[64,128]{1,0:T(8,128)(2,1)S(1)} %get-tuple-element.54), channel_id=1, source_target_pairs={{0,16},{8,24},{16,0},{24,8},{1,17},{9,25},{17,1},{25,9},{2,18},{10... | collective-permute-start | bytes 49160 | tf_op jit(solution)/shard_map/ppermute | solution.py:20
  79.5 4.7 %collective-permute-start.4 = (bf16[64,128]{1,0:T(8,128)(2,1)S(1)}, bf16[64,128]{1,0:T(8,128)(2,1)S(1)}, u32[]{:S(2)}, u32[]{:S(2)}) collective-permute-start(bf16[64,128]{1,0:T(8,128)(2,1)S(1)} %get-tuple-element.55), channel_id=1, source_target_pairs={{0,8},{8,0},{16,24},{24,16},{1,9},{9,1},{17,25},{25,17},{2,10},{10... | collective-permute-start | bytes 49160 | tf_op jit(solution)/shard_map/ppermute | solution.py:20
  81.0 5.5 %collective-permute-start.5 = (bf16[64,128]{1,0:T(8,128)(2,1)S(1)}, bf16[64,128]{1,0:T(8,128)(2,1)S(1)}, u32[]{:S(2)}, u32[]{:S(2)}) collective-permute-start(bf16[64,128]{1,0:T(8,128)(2,1)S(1)} %get-tuple-element.56), channel_id=1, source_target_pairs={{0,24},{8,16},{16,8},{24,0},{1,25},{9,17},{17,9},{25,1},{2,26},{10... | collective-permute-start | bytes 49160 | tf_op jit(solution)/shard_map/ppermute | solution.py:20

commit v3 on v2

--- a/solution.py
+++ b/solution.py
@@ -66,7 +66,7 @@
         if gathered_ref.dtype == f32:
             blocks.append(gathered_ref[d, 0:8])
         else:
-            parts = gathered_ref[d, 0:32].astype(f32)
+            parts = gathered_ref[d, 0:24].astype(f32)
             blocks.append(parts[0:8] + parts[8:16] + parts[16:24])
     return blocks
 
@@ -170,7 +170,7 @@
             tall_ref[pl.ds(at, rows), :] = planes_ref[start + c].astype(f32)
             return carry
 
-        lax.fori_loop(0, block, spill, 0, unroll=8)
+        lax.fori_loop(0, block, spill, 0, unroll=block)
 
         def collect(h, carry, start=start):
             line = tall_ref[pl.ds(h, block, stride=rows), :]
@@ -291,7 +291,7 @@
     both = jnp.zeros((2 * depth, cols), f32)
     total, turned = lax.fori_loop(0, rows, activate, (zero, both), unroll=rows)
     gram = jnp.zeros((depth, 3 * depth), f32)
-    step = 8
+    step = rows
     for h in range(0, rows, step):
         lines = range(h, min(h + step, rows))
         left = jnp.concatenate([centred_ref[k] for k in lines], axis=1)
@@ -318,7 +318,7 @@
     high = block.astype(bf16).astype(f32)
     middle = (block - high).astype(bf16).astype(f32)
     low = block - high - middle
-    block = jnp.concatenate([high, middle, low, jnp.zeros((8, width), f32), across], axis=0)
+    block = jnp.concatenate([high, middle, low, across], axis=0)
     block = block.astype(bf16)
     for d in range(out_ref.shape[0]):
         out_ref[d] = block
@@ -417,9 +417,9 @@
     lift = 0.5 * shift1
     middle = (lift + lift * jnp.tanh(lift)).astype(bf16).astype(f32)
     level_row = level_row + jnp.sum(mixer * middle, axis=0, keepdims=True)
-    across = stat3_ref[0, 32 : 32 + depth].astype(f32)
+    across = stat3_ref[0, 24 : 24 + depth].astype(f32)
     for d in range(1, devices):
-        across = across + stat3_ref[d, 32 : 32 + depth].astype(f32)
+        across = across + stat3_ref[d, 24 : 24 + depth].astype(f32)
     turned = summed_block(stat3_ref)[2 * steps : 2 * steps + 1]
     double = jnp.concatenate([mixer, mixer], axis=1)
     sums_one = sums[2 * steps : 2 * steps + 1] - jnp.sum(double * across, axis=0, keepdims=True)
@@ -472,7 +472,7 @@
 
     lax.fori_loop(0, rows, fill, 0, unroll=rows)
     tall = 3 * depth
-    step = 6
+    step = rows + 2
     grad = jnp.zeros((tall, tall), f32)
     for start in range(0, rows + 2, step):
         lines = range(start, min(start + step, rows + 2))
@@ -607,7 +607,7 @@
     stat_one = swap(stat, group_axes)
     hidden, turn, stat, mixed, mean_y = call(
         hidden_kernel, HIDDEN,
-        [(plane, bf16), ((rows, 2 * depth, cols), bf16), ((group, 32 + depth, 128), bf16)]
+        [(plane, bf16), ((rows, 2 * depth, cols), bf16), ((group, 24 + depth, 128), bf16)]
         + [((depth, wide), f32), ((depth, cols), f32)],
         conv_out, stat_one, *one, proj_weight,
         scratch=[pltpu.VMEM(plane, bf16)],

time: 90.3 us -> 90.9 us (level)
    unnamed x53 -> x49, local copies, waits for them, and re-layouts: 16 us -> 16.7 us
where the time goes in v3:
time: 90.9 us; the launch traced here: 90.1 us
  blocking collectives  29.4 us (32%)
  local copies, waits for them, and re-layouts  16.7 us (18%)
  starting transfers between devices  16.1 us (18%)
  Pallas kernels  14.7 us (16%)
  waiting for transfers between devices  12.3 us (14%)
    all_to_all x3, blocking collectives, swap(): return lax.all_to_all(copies, axes, 0, 0)  29.4 us
    unnamed x49, local copies, waits for them, and re-layouts  16.7 us
    pallas_call x12, Pallas kernels, call(): pl.pallas_call(kernel, out_shape=[jax.ShapeDtypeStruct(s, d) for s, d in...  14.7 us
    ppermute x6, starting transfers between devices, from_partner(): lax.ppermute(value, 'sp', [(i, i ^ mask) for i in range(lax.axis_size('sp...  10.2 us
    ppermute x6, waiting for transfers between devices, from_partner(): lax.ppermute(value, 'sp', [(i, i ^ mask) for i in range(lax.axis_size('sp...  7.63 us
    all_to_all x2, starting transfers between devices, swap(): return lax.all_to_all(copies, axes, 0, 0)  5.96 us
    all_to_all x2, waiting for transfers between devices, swap(): return lax.all_to_all(copies, axes, 0, 0)  4.71 us
  transfers between devices with their start and end apart: 8, of which 4 were waited for; matrix products, arithmetic and copies ran while one was open for 1% of the time, Pallas kernels for 3%

profile of v3, /device:TPU:0, one launch (start us, length us, event | category | flops | bytes accessed | tf_op | source)
XLA Modules:
  0.0 90.1 jit_solution(10890628837406171008)
XLA Ops:
  0.6 0.0 copy-start.7
  0.6 1.1 %copy-done.7 = bf16[1,1,64,40,128]{4,3,2,1,0:T(8,128)(2,1)S(1)} copy-done((bf16[1,1,64,40,128]{4,3,2,1,0:T(8,128)(2,1)S(1)}, bf16[1,1,64,40,128]{4,3,2,1,0:T(8,128)(2,1)}, u32[]{:S(2)}) %copy-start.7) | copy-done | bytes 655384
  1.7 0.4 shard_map.135
  2.1 4.1 %collective-permute-start = (bf16[64,128]{1,0:T(8,128)(2,1)S(1)}, bf16[64,128]{1,0:T(8,128)(2,1)S(1)}, u32[]{:S(2)}, u32[]{:S(2)}) collective-permute-start(bf16[64,128]{1,0:T(8,128)(2,1)S(1)} %get-tuple-element.38), channel_id=1, source_target_pairs={{0,16},{8,24},{16,0},{24,8},{1,17},{9,25},{17,1},{25,9},{2,18},{10... | collective-permute-start | bytes 49160 | tf_op jit(solution)/shard_map/ppermute | solution.py:20
  6.2 1.6 %collective-permute-start.1 = (bf16[64,128]{1,0:T(8,128)(2,1)S(1)}, bf16[64,128]{1,0:T(8,128)(2,1)S(1)}, u32[]{:S(2)}, u32[]{:S(2)}) collective-permute-start(bf16[64,128]{1,0:T(8,128)(2,1)S(1)} %get-tuple-element.39), channel_id=1, source_target_pairs={{0,8},{8,0},{16,24},{24,16},{1,9},{9,1},{17,25},{25,17},{2,10},{10... | collective-permute-start | bytes 49160 | tf_op jit(solution)/shard_map/ppermute | solution.py:20
  7.8 0.0 collective-permute-start.2
  7.8 0.0 copy-start.8
  7.8 0.8 copy-done.8
  8.6 0.0 copy-start.13
  8.6 0.9 %copy-done.13 = bf16[3,3,64,64]{3,2,1,0:T(8,128)(2,1)S(1)} copy-done((bf16[3,3,64,64]{3,2,1,0:T(8,128)(2,1)S(1)}, bf16[3,3,64,64]{3,2,1,0:T(8,128)(2,1)}, u32[]{:S(2)}) %copy-start.13) | copy-done | bytes 73752
  9.5 0.3 shard_map.136
  9.7 0.0 copy-start.11
  9.7 0.7 copy-done.11
  10.4 0.0 copy-start.14
  10.4 0.6 copy-done.14
  11.0 0.0 collective-permute-done.row_ref
  11.0 0.0 collective-permute-done.1.col_ref
  11.0 2.3 %collective-permute-done.2.corner_ref = bf16[64,128]{1,0:T(8,128)(2,1)S(1)} collective-permute-done((bf16[64,128]{1,0:T(8,128)(2,1)S(1)}, bf16[64,128]{1,0:T(8,128)(2,1)S(1)}, u32[]{:S(2)}, u32[]{:S(2)}) %collective-permute-start.2) | collective-permute-done | bytes 16416 | tf_op jit(solution)/shard_map/ppermute | solution.py:20
  13.3 1.2 %shard_map.137 = (bf16[42,192,128]{2,1,0:T(8,128)(2,1)S(1)}, f32[40,64,128]{2,1,0:T(8,128)S(1)}, f32[8,8,128]{2,1,0:T(8,128)S(1)}) custom-call(bf16[40,64,128]{2,1,0:T(8,128)(2,1)S(1)} %get-tuple-element.37.x_ref, bf16[64,128]{1,0:T(8,128)(2,1)S(1)} %collective-permute-done.row_ref, bf16[64,128]{1,0:T(8,128)(2,1)S(1)} %collective-permute-done.1.col_ref, ...), custom_call_target="tpu_custom_call" | custom-call | tf_op jit(solution)/shard_map/pallas_call | solution.py:559
  14.6 0.0 copy-start.3
  14.6 1.4 %copy-done.3 = bf16[42,192,128]{2,1,0:T(8,128)(2,1)} copy-done((bf16[42,192,128]{2,1,0:T(8,128)(2,1)}, bf16[42,192,128]{2,1,0:T(8,128)(2,1)S(1)}, u32[]{:S(2)}) %copy-start.3) | copy-done | bytes 2064408
  15.9 10.2 %all_to_all.25.stat_ref.stat1_ref = f32[8,8,128]{2,1,0:T(8,128)S(1)} all-to-all(f32[8,8,128]{2,1,0:T(8,128)S(1)} %get-tuple-element.43), channel_id=1, replica_groups=mesh['sp'=4,'bn'=2,'dp'=4] {'sp','bn'}, dimensions={0} | all-to-all | bytes 65536 | tf_op jit(solution)/shard_map/all_to_all | solution.py:572
  26.1 0.8 copy-done.9
  26.9 0.7 copy-done.19
  27.6 0.7 copy-done.21
  28.2 2.9 %shard_map.138 = (bf16[40,64,128]{2,1,0:T(8,128)(2,1)S(1)}, bf16[40,128,128]{2,1,0:T(8,128)(2,1)S(1)}, bf16[8,88,128]{2,1,0:T(8,128)(2,1)}, f32[64,256]{1,0:T(8,128)S(1)}, f32[64,128]{1,0:T(8,128)S(1)}) custom-call(f32[40,64,128]{2,1,0:T(8,128)S(1)} %get-tuple-element.42.a_ref, f32[8,8,128]{2,1,0:T(8,128)S(1)} %all_to_all.25.stat_ref.stat1_ref, ...), custom_call_target="tpu_custom_call" | custom-call | tf_op jit(solution)/shard_map/pallas_call | solution.py:559
  31.1 1.1 %copy-done = f32[40,64,128]{2,1,0:T(8,128)} copy-done((f32[40,64,128]{2,1,0:T(8,128)}, f32[40,64,128]{2,1,0:T(8,128)S(1)}, u32[]{:S(2)}) %copy-start) | copy-done | bytes 1310744
  32.1 1.0 %copy-done.5 = bf16[40,128,128]{2,1,0:T(8,128)(2,1)} copy-done((bf16[40,128,128]{2,1,0:T(8,128)(2,1)}, bf16[40,128,128]{2,1,0:T(8,128)(2,1)S(1)}, u32[]{:S(2)}) %copy-start.5) | copy-done | bytes 1310744
  33.2 0.6 copy-done.16
  33.8 3.4 %all-to-all-start.1 = ((bf16[8,88,128]{2,1,0:T(8,128)(2,1)}), bf16[8,88,128]{2,1,0:T(8,128)(2,1)S(1)}, u32[]{:S(2)}, u32[]{:S(2)}) async-start(bf16[8,88,128]{2,1,0:T(8,128)(2,1)} %get-tuple-element.46), calls=%async_computation.1 | async-start | bytes 360448 | tf_op jit(solution)/shard_map/all_to_all | solution.py:572
  37.2 0.0 copy-start.2
  37.2 1.7 %copy-done.2 = bf16[1,1,256,40,128]{4,3,2,1,0:T(8,128)(2,1)S(1)} copy-done((bf16[1,1,256,40,128]{4,3,2,1,0:T(8,128)(2,1)S(1)}, bf16[1,1,256,40,128]{4,3,2,1,0:T(8,128)(2,1)}, u32[]{:S(2)}) %copy-start.2) | copy-done | bytes 2621464
  38.9 1.2 %shard_map.139.g_ref = bf16[40,256,128]{2,1,0:T(8,128)(2,1)S(1)} custom-call(bf16[256,40,128]{2,1,0:T(8,128)(2,1)S(1)} %bitcast.15), custom_call_target="tpu_custom_call" | custom-call | tf_op jit(solution)/shard_map/pallas_call | solution.py:559
  40.1 4.7 %all-to-all-done.1.stat_ref.stat3_ref = bf16[8,88,128]{2,1,0:T(8,128)(2,1)S(1)} async-done(((bf16[8,88,128]{2,1,0:T(8,128)(2,1)}), bf16[8,88,128]{2,1,0:T(8,128)(2,1)S(1)}, u32[]{:S(2)}, u32[]{:S(2)}) %all-to-all-start.1) | async-done | bytes 180256 | tf_op jit(solution)/shard_map/all_to_all | solution.py:572
  44.8 0.0 copy-done.10
  44.8 1.3 %copy-done.6 = bf16[40,128,128]{2,1,0:T(8,128)(2,1)S(1)} copy-done((bf16[40,128,128]{2,1,0:T(8,128)(2,1)S(1)}, bf16[40,128,128]{2,1,0:T(8,128)(2,1)}, u32[]{:S(2)}) %copy-start.6) | copy-done | bytes 1310744
  46.1 0.8 copy-done.15
  47.0 0.7 copy-done.18
  47.6 0.7 copy-done.23
  48.3 4.2 %shard_map.140 = (f32[40,64,128]{2,1,0:T(8,128)S(1)}, f32[64,256]{1,0:T(8,128)S(1)}, f32[8,8,128]{2,1,0:T(8,128)S(1)}) custom-call(bf16[40,64,128]{2,1,0:T(8,128)(2,1)S(1)} %get-tuple-element.44.y_ref, bf16[40,256,128]{2,1,0:T(8,128)(2,1)S(1)} %shard_map.139.g_ref, bf16[40,128,128]{2,1,0:T(8,128)(2,1)S(1)} %copy-done.6, ...), custom_call_target="tpu_custom_call" | custom-call | tf_op jit(solution)/shard_map/pallas_call | solution.py:559
  52.5 0.0 copy-start.4
  52.5 9.2 %all_to_all.26.sums_ref = f32[8,8,128]{2,1,0:T(8,128)S(1)} all-to-all(f32[8,8,128]{2,1,0:T(8,128)S(1)} %get-tuple-element.49), channel_id=1, replica_groups=mesh['sp'=4,'bn'=2,'dp'=4] {'sp','bn'}, dimensions={0} | all-to-all | bytes 65536 | tf_op jit(solution)/shard_map/all_to_all | solution.py:572
  61.7 0.0 copy-done.1
  61.7 0.0 copy-done.17
  61.7 0.0 copy-done.20
  61.7 0.0 copy-done.22
  61.7 1.5 %shard_map.141 = (bf16[40,64,128]{2,1,0:T(8,128)(2,1)S(1)}, bf16[64,128]{1,0:T(8,128)(2,1)S(1)}, bf16[64,128]{1,0:T(8,128)(2,1)S(1)}, bf16[64,128]{1,0:T(8,128)(...) custom-call(bf16[40,64,128]{2,1,0:T(8,128)(2,1)S(1)} %get-tuple-element.44.y_ref, ...), custom_call_target="tpu_custom_call" | custom-call | tf_op jit(solution)/shard_map/pallas_call | solution.py:559
  63.2 0.0 copy-start.12
  63.2 0.0 copy-done.4
  63.3 0.8 shard_map.144
  64.1 10.0 %all_to_all.27.parts_ref = bf16[32,16,128]{2,1,0:T(8,128)(2,1)S(1)} all-to-all(bf16[32,16,128]{2,1,0:T(8,128)(2,1)S(1)} %bitcast.18), channel_id=1, replica_groups=mesh['sp'=4,'bn'=2,'dp'=4] {'sp','bn','dp'}, dimensions={0} | all-to-all | bytes 262144 | tf_op jit(solution)/shard_map/all_to_all | solution.py:572
  74.1 0.7 shard_map.145
  74.8 2.6 %all-to-all-start.4 = ((bf16[32,16,128]{2,1,0:T(8,128)(2,1)}), bf16[32,16,128]{2,1,0:T(8,128)(2,1)S(1)}, u32[]{:S(2)}, u32[]{:S(2)}) async-start(bf16[32,16,128]{2,1,0:T(8,128)(2,1)} %shard_map.145), calls=%async_computation.4 | async-start | bytes 262144 | tf_op jit(solution)/shard_map/all_to_all | solution.py:572
  77.3 2.7 %collective-permute-start.3 = (bf16[64,128]{1,0:T(8,128)(2,1)S(1)}, bf16[64,128]{1,0:T(8,128)(2,1)S(1)}, u32[]{:S(2)}, u32[]{:S(2)}) collective-permute-start(bf16[64,128]{1,0:T(8,128)(2,1)S(1)} %get-tuple-element.54), channel_id=1, source_target_pairs={{0,16},{8,24},{16,0},{24,8},{1,17},{9,25},{17,1},{25,9},{2,18},{10... | collective-permute-start | bytes 49160 | tf_op jit(solution)/shard_map/ppermute | solution.py:20
  80.1 1.5 %collective-permute-start.4 = (bf16[64,128]{1,0:T(8,128)(2,1)S(1)}, bf16[64,128]{1,0:T(8,128)(2,1)S(1)}, u32[]{:S(2)}, u32[]{:S(2)}) collective-permute-start(bf16[64,128]{1,0:T(8,128)(2,1)S(1)} %get-tuple-element.55), channel_id=1, source_target_pairs={{0,8},{8,0},{16,24},{24,16},{1,9},{9,1},{17,25},{25,17},{2,10},{10... | collective-permute-start | bytes 49160 | tf_op jit(solution)/shard_map/ppermute | solution.py:20
  81.6 0.2 collective-permute-start.5
  81.8 3.0 %collective-permute-done.3.row_ref = bf16[64,128]{1,0:T(8,128)(2,1)S(1)} collective-permute-done((bf16[64,128]{1,0:T(8,128)(2,1)S(1)}, bf16[64,128]{1,0:T(8,128)(2,1)S(1)}, u32[]{:S(2)}, u32[]{:S(2)}) %collective-permute-start.3) | collective-permute-done | bytes 16416 | tf_op jit(solution)/shard_map/ppermute | solution.py:20
  84.7 0.0 collective-permute-done.4.col_ref
  84.7 2.4 %collective-permute-done.5.corner_ref = bf16[64,128]{1,0:T(8,128)(2,1)S(1)} collective-permute-done((bf16[64,128]{1,0:T(8,128)(2,1)S(1)}, bf16[64,128]{1,0:T(8,128)(2,1)S(1)}, u32[]{:S(2)}, u32[]{:S(2)}) %collective-permute-start.5) | collective-permute-done | bytes 16416 | tf_op jit(solution)/shard_map/ppermute | solution.py:20
  87.1 0.0 copy-done.12
  87.1 0.9 %shard_map.143 = bf16[40,64,128]{2,1,0:T(8,128)(2,1)S(1)} custom-call(bf16[40,64,128]{2,1,0:T(8,128)(2,1)S(1)} %get-tuple-element.53.d_ref.da_ref, bf16[2,64,128]{2,1,0:T(8,128)(2,1)S(1)} %shard_map.142.beside_ref, bf16[128,768]{1,0:T(8,128)(2,1)S(1)} %copy-done.12), custom_call_target="tpu_custom_call" | custom-call | tf_op jit(solution)/shard_map/pallas_call | solution.py:559
  88.0 1.3 %copy.15 = bf16[1,1,64,40,128]{4,3,2,1,0:T(8,128)(2,1)} copy(bf16[1,1,64,40,128]{4,2,3,1,0:T(8,128)(2,1)S(1)} %bitcast.16) | data formatting | bytes 1310720
  89.3 0.0 all-to-all-done.4
  89.3 0.8 shard_map.146
  (16 shorter events, 0.0 us)
Async XLA Ops:
  0.6 1.1 %copy-start.7 = (bf16[1,1,64,40,128]{4,3,2,1,0:T(8,128)(2,1)S(1)}, bf16[1,1,64,40,128]{4,3,2,1,0:T(8,128)(2,1)}, u32[]{:S(2)}) copy-start(bf16[1,1,64,40,128]{4,3,2,1,0:T(8,128)(2,1)} %param.8) | copy-start | bytes 1966084
  2.1 9.0 %collective-permute-start = (bf16[64,128]{1,0:T(8,128)(2,1)S(1)}, bf16[64,128]{1,0:T(8,128)(2,1)S(1)}, u32[]{:S(2)}, u32[]{:S(2)}) collective-permute-start(bf16[64,128]{1,0:T(8,128)(2,1)S(1)} %get-tuple-element.38), channel_id=1, source_target_pairs={{0,16},{8,24},{16,0},{24,8},{1,17},{9,25},{17,1},{25,9},{2,18},{10... | collective-permute-start | bytes 49160 | tf_op jit(solution)/shard_map/ppermute | solution.py:20
  6.2 4.8 %collective-permute-start.1 = (bf16[64,128]{1,0:T(8,128)(2,1)S(1)}, bf16[64,128]{1,0:T(8,128)(2,1)S(1)}, u32[]{:S(2)}, u32[]{:S(2)}) collective-permute-start(bf16[64,128]{1,0:T(8,128)(2,1)S(1)} %get-tuple-element.39), channel_id=1, source_target_pairs={{0,8},{8,0},{16,24},{24,16},{1,9},{9,1},{17,25},{25,17},{2,10},{10... | collective-permute-start | bytes 49160 | tf_op jit(solution)/shard_map/ppermute | solution.py:20
  7.8 5.5 %collective-permute-start.2 = (bf16[64,128]{1,0:T(8,128)(2,1)S(1)}, bf16[64,128]{1,0:T(8,128)(2,1)S(1)}, u32[]{:S(2)}, u32[]{:S(2)}) collective-permute-start(bf16[64,128]{1,0:T(8,128)(2,1)S(1)} %get-tuple-element.40), channel_id=1, source_target_pairs={{0,24},{8,16},{16,8},{24,0},{1,25},{9,17},{17,9},{25,1},{2,26},{10... | collective-permute-start | bytes 49160 | tf_op jit(solution)/shard_map/ppermute | solution.py:20
  7.8 0.8 copy-start.8
  8.6 0.9 %copy-start.13 = (bf16[3,3,64,64]{3,2,1,0:T(8,128)(2,1)S(1)}, bf16[3,3,64,64]{3,2,1,0:T(8,128)(2,1)}, u32[]{:S(2)}) copy-start(bf16[3,3,64,64]{3,2,1,0:T(8,128)(2,1)} %conv_ref.1) | copy-start | bytes 221188
  9.7 0.7 copy-start.11
  10.4 0.6 copy-start.14
  14.6 1.4 %copy-start.3 = (bf16[42,192,128]{2,1,0:T(8,128)(2,1)}, bf16[42,192,128]{2,1,0:T(8,128)(2,1)S(1)}, u32[]{:S(2)}) copy-start(bf16[42,192,128]{2,1,0:T(8,128)(2,1)S(1)} %get-tuple-element.58.shifted_ref) | copy-start | bytes 6193156
  26.1 0.8 copy-start.9
  26.9 0.7 copy-start.19
  27.5 0.7 copy-start.21
  31.1 1.1 %copy-start = (f32[40,64,128]{2,1,0:T(8,128)}, f32[40,64,128]{2,1,0:T(8,128)S(1)}, u32[]{:S(2)}) copy-start(f32[40,64,128]{2,1,0:T(8,128)S(1)} %get-tuple-element.42.a_ref) | copy-start | bytes 3932164
  32.1 1.1 %copy-start.5 = (bf16[40,128,128]{2,1,0:T(8,128)(2,1)}, bf16[40,128,128]{2,1,0:T(8,128)(2,1)S(1)}, u32[]{:S(2)}) copy-start(bf16[40,128,128]{2,1,0:T(8,128)(2,1)S(1)} %get-tuple-element.45.turn_ref) | copy-start | bytes 3932164
  33.2 0.6 copy-start.16
  33.8 11.0 %all-to-all-start.1 = ((bf16[8,88,128]{2,1,0:T(8,128)(2,1)}), bf16[8,88,128]{2,1,0:T(8,128)(2,1)S(1)}, u32[]{:S(2)}, u32[]{:S(2)}) async-start(bf16[8,88,128]{2,1,0:T(8,128)(2,1)} %get-tuple-element.46), calls=%async_computation.1 | async-start | bytes 360448 | tf_op jit(solution)/shard_map/all_to_all | solution.py:572
  37.2 1.7 %copy-start.2 = (bf16[1,1,256,40,128]{4,3,2,1,0:T(8,128)(2,1)S(1)}, bf16[1,1,256,40,128]{4,3,2,1,0:T(8,128)(2,1)}, u32[]{:S(2)}) copy-start(bf16[1,1,256,40,128]{4,3,2,1,0:T(8,128)(2,1)} %param.9) | copy-start | bytes 7864324
  38.9 5.9 %copy-start.10 = (bf16[64,256]{1,0:T(8,128)(2,1)S(1)}, bf16[64,256]{1,0:T(8,128)(2,1)}, u32[]{:S(2)}) copy-start(bf16[64,256]{1,0:T(8,128)(2,1)} %wt_ref.3) | copy-start | bytes 98308
  44.8 1.3 %copy-start.6 = (bf16[40,128,128]{2,1,0:T(8,128)(2,1)S(1)}, bf16[40,128,128]{2,1,0:T(8,128)(2,1)}, u32[]{:S(2)}) copy-start(bf16[40,128,128]{2,1,0:T(8,128)(2,1)} %copy-done.5) | copy-start | bytes 3932164
  46.1 0.8 copy-start.15
  47.0 0.7 copy-start.18
  47.6 0.7 copy-start.23
  48.3 13.4 %copy-start.1 = (f32[40,64,128]{2,1,0:T(8,128)S(1)}, f32[40,64,128]{2,1,0:T(8,128)}, u32[]{:S(2)}) copy-start(f32[40,64,128]{2,1,0:T(8,128)} %copy-done) | copy-start | bytes 3932164
  48.3 13.4 %copy-start.17 = (f32[64,256]{1,0:T(8,128)S(1)}, f32[64,256]{1,0:T(8,128)}, u32[]{:S(2)}) copy-start(f32[64,256]{1,0:T(8,128)} %copy-done.16) | copy-start | bytes 196612
  48.3 13.4 %copy-start.20 = (f32[64]{0:T(128)S(1)}, f32[64]{0:T(128)}, u32[]{:S(2)}) copy-start(f32[64]{0:T(128)} %param.12) | copy-start | bytes 772
  48.3 13.4 %copy-start.22 = (f32[64]{0:T(128)S(1)}, f32[64]{0:T(128)}, u32[]{:S(2)}) copy-start(f32[64]{0:T(128)} %param.13) | copy-start | bytes 772
  52.5 10.7 %copy-start.4 = (bf16[42,192,128]{2,1,0:T(8,128)(2,1)S(1)}, bf16[42,192,128]{2,1,0:T(8,128)(2,1)}, u32[]{:S(2)}) copy-start(bf16[42,192,128]{2,1,0:T(8,128)(2,1)} %copy-done.3) | copy-start | bytes 6193156
  63.2 23.9 %copy-start.12 = (bf16[128,768]{1,0:T(8,128)(2,1)S(1)}, bf16[128,768]{1,0:T(8,128)(2,1)}, u32[]{:S(2)}) copy-start(bf16[128,768]{1,0:T(8,128)(2,1)} %copy-done.11) | copy-start | bytes 589828
  74.8 14.6 %all-to-all-start.4 = ((bf16[32,16,128]{2,1,0:T(8,128)(2,1)}), bf16[32,16,128]{2,1,0:T(8,128)(2,1)S(1)}, u32[]{:S(2)}, u32[]{:S(2)}) async-start(bf16[32,16,128]{2,1,0:T(8,128)(2,1)} %shard_map.145), calls=%async_computation.4 | async-start | bytes 262144 | tf_op jit(solution)/shard_map/all_to_all | solution.py:572
  77.3 7.4 %collective-permute-start.3 = (bf16[64,128]{1,0:T(8,128)(2,1)S(1)}, bf16[64,128]{1,0:T(8,128)(2,1)S(1)}, u32[]{:S(2)}, u32[]{:S(2)}) collective-permute-start(bf16[64,128]{1,0:T(8,128)(2,1)S(1)} %get-tuple-element.54), channel_id=1, source_target_pairs={{0,16},{8,24},{16,0},{24,8},{1,17},{9,25},{17,1},{25,9},{2,18},{10... | collective-permute-start | bytes 49160 | tf_op jit(solution)/shard_map/ppermute | solution.py:20
  80.1 4.7 %collective-permute-start.4 = (bf16[64,128]{1,0:T(8,128)(2,1)S(1)}, bf16[64,128]{1,0:T(8,128)(2,1)S(1)}, u32[]{:S(2)}, u32[]{:S(2)}) collective-permute-start(bf16[64,128]{1,0:T(8,128)(2,1)S(1)} %get-tuple-element.55), channel_id=1, source_target_pairs={{0,8},{8,0},{16,24},{24,16},{1,9},{9,1},{17,25},{25,17},{2,10},{10... | collective-permute-start | bytes 49160 | tf_op jit(solution)/shard_map/ppermute | solution.py:20
  81.6 5.5 %collective-permute-start.5 = (bf16[64,128]{1,0:T(8,128)(2,1)S(1)}, bf16[64,128]{1,0:T(8,128)(2,1)S(1)}, u32[]{:S(2)}, u32[]{:S(2)}) collective-permute-start(bf16[64,128]{1,0:T(8,128)(2,1)S(1)} %get-tuple-element.56), channel_id=1, source_target_pairs={{0,24},{8,16},{16,8},{24,0},{1,25},{9,17},{17,9},{25,1},{2,26},{10... | collective-permute-start | bytes 49160 | tf_op jit(solution)/shard_map/ppermute | solution.py:20
